TPU v7x, 256 devices: a whole 4x4x8 slice. The times are simulated.
256 devices in a mesh: pairs: 32 (over x, y, core), aux: 8 (over z).
Axes of the slice: x: 4, y: 4, z: 8, core: 2. Of those that a mesh axis runs over, the one named last changes fastest.
Arguments:
- panels: bfloat16 [64, 28672, 256], P(None, ('pairs', 'aux')), may hold values from -0.59765625 to 0.59765625
- domain: int32 [32, 6], replicated, may hold values from 0 to 63, as said below
- pair_slots: int32 [384, 2], P('pairs'), may hold values from 0 to 5
- ranks: int32 [384, 2], P('pairs'), may hold values from 40 to 128
- transforms: bfloat16 [384, 2, 256, 128], P('pairs'), may hold values from -0.375 to 0.375
- trial: bfloat16 [384, 2, 128, 128], P('pairs'), may hold values from -0.5 to 0.5
Outputs:
- sigma: bfloat16 [384, 2, 128, 128], P('pairs', None, 'aux')
Inputs may be any that keep to these rules, and one draw needn't show every extreme that they name: `domain`: each row holds 6 different LMO numbers.
All inputs are finite; a program needn't handle non-finite values.
Results may differ from a plain program's by a relative error of at most 0.0039.
Values may be sent and summed in bfloat16 or wider, within the bound.
No kernel may reach another device: no remote copies, remote signals or barrier semaphores. Data moves between devices by JAX's collectives and lax.ppermute only.
A program may use at most 128 MiB of HBM per device.

v0:
```python
import functools

import jax
import jax.numpy as jnp
import numpy as np
from jax import lax
from jax.experimental import pallas as pl
from jax.experimental.pallas import tpu as pltpu
from jax.sharding import PartitionSpec as P


SIDE = 4
BATCHES = ((8,), (6, 2))

STEPS = (
    ((0, 0), (1, 0), (-1, 0), (0, 1), (0, -1), (-1, -1), (-1, 1), (2, 0)),
    ((0, 0), (1, 0), (-1, 0), (0, 1), (0, -1), (1, 1), (1, -1), (0, 2)),
)


def place(x, y, core):
    return ((x % SIDE) * SIDE + y % SIDE) * 2 + core


def permutation(move):
    return [
        (place(x, y, core), place(*move(x, y, core))) for x in range(SIDE) for y in range(SIDE) for core in (0, 1)
    ]


def plan():
    perms, targets = [], []
    for step in range(len(STEPS[0])):
        perm = permutation(lambda x, y, t: (x + STEPS[t][step][0], y + STEPS[t][step][1], t))
        own = dict(perm)
        partner = dict(permutation(lambda x, y, t: (x + STEPS[t][step][0] + 2, y + STEPS[t][step][1] + 2, t)))
        perms.append(perm)
        targets.append([(partner[device], own[device]) for device in range(len(perm))])
    return perms, np.asarray(targets, np.int32).transpose(1, 2, 0)


def collect_kernel(rows_ref, panels_ref, sibling_ref, *refs):
    outs, sems = refs[:-1], refs[-1]
    slots = rows_ref.shape[1]
    copies = []
    for step, out_ref in enumerate(outs):
        for slot in range(slots):
            for half, source_ref in enumerate((panels_ref, sibling_ref)):
                copies.append(
                    pltpu.make_async_copy(
                        source_ref.at[rows_ref[step, slot]],
                        out_ref.at[half * slots + slot],
                        sems.at[(step * slots + slot) * 2 + half],
                    )
                )
    for copy in copies:
        copy.start()
    for copy in copies:
        copy.wait()


def collect(rows, panels, sibling):
    steps, slots = rows.shape
    anywhere = pl.BlockSpec(memory_space=pl.ANY)
    block = jax.ShapeDtypeStruct((2 * slots,) + panels.shape[1:], panels.dtype)
    return pl.pallas_call(
        collect_kernel,
        out_shape=[block] * steps,
        in_specs=[pl.BlockSpec(memory_space=pltpu.SMEM), anywhere, anywhere],
        out_specs=[anywhere] * steps,
        scratch_shapes=[pltpu.SemaphoreType.DMA((steps * slots * 2,))],
    )(rows, panels, sibling)


def dot(a, b, dims=(((1,), (0,)), ((), ()))):
    return lax.dot_general(a, b, dims, preferred_element_type=jnp.float32)


def contribution(lefts, rights, coeffs):
    left = dot(jnp.concatenate(lefts, axis=0), coeffs).astype(jnp.bfloat16)
    right = dot(jnp.concatenate(rights, axis=0), coeffs).astype(jnp.bfloat16)
    r = coeffs.shape[1] // 2
    tn = (((0,), (0,)), ((), ()))
    return [dot(left[:, s], right[:, s], tn) for s in (slice(0, r), slice(r, 2 * r))]


def dress(k, amplitude):
    high = k.astype(jnp.bfloat16)
    low = (k - high.astype(jnp.float32)).astype(jnp.bfloat16)
    both = jnp.concatenate([high, low], axis=0)
    n = k.shape[0]
    with_right = dot(both, amplitude)
    with_left = dot(amplitude, both, (((1,), (1,)), ((), ())))
    return k + (with_right[:n] + with_right[n:]) + (with_left[:, :n] + with_left[:, n:])


def kernel(count, first, last, pieces, slots_ref, w_ref, *refs):
    blocks = refs[:count]
    out_ref = refs[-1]
    v = w_ref.shape[1] - w_ref.shape[2]

    slots = blocks[0].shape[0] // 2

    def pair(p, carry):
        i, j = slots_ref[p, 0], slots_ref[p, 1]
        coeffs = jnp.concatenate([w_ref[2 * p, :v, :], w_ref[2 * p + 1, :v, :]], axis=1)
        lefts = [b[half * slots + i] for b in blocks for half in range(2)]
        rights = [b[half * slots + j] for b in blocks for half in range(2)]
        total = contribution(lefts, rights, coeffs)
        for root in range(2):
            k = total[root]
            if not first:
                k = k + refs[count][2 * p + root]
            if last:
                sigma = dress(k, w_ref[2 * p + root, v:, :]).astype(jnp.bfloat16)
                rows = sigma.shape[0] // pieces
                for piece in range(pieces):
                    out_ref[piece, 2 * p + root] = sigma[piece * rows : (piece + 1) * rows]
            else:
                out_ref[2 * p + root] = k
        return carry

    lax.fori_loop(0, slots_ref.shape[0], pair, 0)


def accumulate(slots, w, blocks, total, last, pieces):
    count, first = len(blocks), total is None
    n, r = w.shape[0], w.shape[2]
    shape = (pieces, n, r // pieces, r) if last else (n, r, r)
    dtype = jnp.bfloat16 if last else jnp.float32
    operands = [w, *blocks] + ([] if first else [total])
    rows = 2 * count * blocks[0].shape[1]
    v = w.shape[1] - r
    vmem = pl.BlockSpec(memory_space=pltpu.VMEM)
    return pl.pallas_call(
        functools.partial(kernel, count, first, last, pieces),
        out_shape=jax.ShapeDtypeStruct(shape, dtype),
        in_specs=[pl.BlockSpec(memory_space=pltpu.SMEM)] + [vmem] * len(operands),
        out_specs=vmem,
        cost_estimate=pl.CostEstimate(
            flops=n * rows * r * (4 * v + 2 * r), bytes_accessed=2 * rows * 6 * v + 4 * n * r * r, transcendentals=0
        ),
    )(slots, *operands)


def per_device(panels, domain, pair_slots, ranks, transforms, trial):
    perms, targets = plan()
    partner = permutation(lambda x, y, core: (x + 2, y + 2, core))
    partner_slots = lax.ppermute(pair_slots, "pairs", partner)
    sibling = lax.ppermute(panels, "pairs", permutation(lambda x, y, core: (x, y, 1 - core)))
    z, pieces = lax.axis_index("aux"), lax.axis_size("aux")
    width = transforms.shape[3]
    keep = lax.broadcasted_iota(jnp.int32, ranks.shape + (width,), 2) < ranks[:, :, None]
    masked_d = jnp.where(keep[:, :, None, :], transforms, jnp.zeros_like(transforms))
    masked_c = jnp.where(keep[:, :, :, None] & keep[:, :, None, :], trial, jnp.zeros_like(trial))
    own_w = jnp.concatenate([masked_d, masked_c], axis=2)
    own_w = own_w.reshape(-1, own_w.shape[2], width)

    share = own_w.shape[0] // pieces
    shard = lax.ppermute(lax.dynamic_slice_in_dim(own_w, z * share, share, 0), "pairs", partner)
    partner_w = lax.all_to_all(
        jnp.broadcast_to(shard[None], (pieces,) + shard.shape), "aux", split_axis=0, concat_axis=0, tiled=True
    ).reshape(own_w.shape)

    mine = jnp.asarray(targets)[lax.axis_index("pairs")]
    rows_of = jnp.take(domain, mine, axis=0, mode="clip")
    arrived = []
    for side in range(2):
        blocks = collect(rows_of[side], panels, sibling)
        row = [blocks[0]]
        for step in range(1, len(perms)):
            row.append(lax.ppermute(blocks[step], "pairs", perms[step]))
        arrived.append(row)

    def sums(side, slots, w):
        total, at = None, 0
        for count in BATCHES[side]:
            last = at + count == len(perms)
            total = accumulate(slots, w, arrived[side][at : at + count], total, last, pieces)
            at += count
        got = lax.all_to_all(total, "aux", split_axis=0, concat_axis=0, tiled=True)
        return got.astype(jnp.float32).sum(axis=0)

    from_partner = lax.ppermute(sums(0, partner_slots, partner_w), "pairs", partner)
    summed = (sums(1, pair_slots, own_w) + from_partner).astype(jnp.bfloat16)
    return summed.reshape(ranks.shape + summed.shape[1:])


def solution(mesh):
    return jax.shard_map(
        per_device,
        mesh=mesh,
        in_specs=(
            P(None, ("pairs", "aux"), None),
            P(),
            P("pairs", None),
            P("pairs", None),
            P("pairs", None, None, None),
            P("pairs", None, None, None),
        ),
        out_specs=P("pairs", None, "aux", None),
        check_vma=False,
    )
```

profile of v0, /device:TPU:12, one launch (start us, length us, event | category | flops | bytes accessed | tf_op | source)
XLA Modules:
  0.0 510.7 jit_solution(17720492178957666981)
XLA Ops:
  0.0 0.9 copy.8
  1.0 1.6 and_select_fusion
  3.0 2.3 collective-permute-start.9
  5.3 11.0 %collective-permute-done.9 = bf16[3,384,128]{2,1,0:T(8,128)(2,1)S(1)} collective-permute-done((bf16[3,384,128]{2,1,0:T(8,128)(2,1)S(1)}, bf16[3,384,128]{2,1,0:T(8,128)(2,1)S(1)}, u32[]{:S(2)}, u32[]{:S(2)}) %collective-permute-start.9) | collective-permute-done | bytes 294944 | tf_op jit(solution)/shard_map/ppermute | solution.py:160
  16.3 2.0 broadcast_in_dim.32
  18.3 8.6 %all-to-all-start.1 = ((bf16[8,3,384,128]{3,2,1,0:T(8,128)(2,1)}), bf16[8,3,384,128]{3,2,1,0:T(8,128)(2,1)}, u32[]{:S(2)}, u32[]{:S(2)}) async-start(bf16[8,3,384,128]{3,2,1,0:T(8,128)(2,1)} %broadcast_in_dim.32), calls=%async_computation.1 | async-start | bytes 4718592 | tf_op jit(solution)/shard_map/all_to_all | solution.py:161
  28.9 169.6 %shard_map.76 = (bf16[12,112,256]{2,1,0:T(8,128)(2,1)}, bf16[12,112,256]{2,1,0:T(8,128)(2,1)}, bf16[12,112,256]{2,1,0:T(8,128)(2,1)}, bf16[12,112,256]{2,1,0:T(8...) custom-call(s32[8,6]{1,0:T(8,128)} %get-tuple-element.37.rows_ref, ...), custom_call_target="tpu_custom_call" | custom-call | tf_op jit(solution)/shard_map/pallas_call | solution.py:66
  198.5 1.3 collective-permute-start.10
  199.8 0.8 collective-permute-start.11
  200.7 3.5 collective-permute-start.8
  204.2 2.0 collective-permute-start.13
  206.2 11.2 %collective-permute-done.8.slots_ref = s32[12,2]{1,0:T(8,128)S(1)} collective-permute-done((s32[12,2]{1,0:T(8,128)S(1)}, s32[12,2]{1,0:T(8,128)S(1)}, u32[]{:S(2)}, u32[]{:S(2)}) %collective-permute-start.8) | collective-permute-done | bytes 128 | tf_op jit(solution)/shard_map/ppermute | solution.py:149
  217.4 3.2 collective-permute-start.14
  220.6 1.0 collective-permute-start.15
  221.6 1.1 collective-permute-start.16
  222.7 169.5 %shard_map.73 = (bf16[12,112,256]{2,1,0:T(8,128)(2,1)}, bf16[12,112,256]{2,1,0:T(8,128)(2,1)}, bf16[12,112,256]{2,1,0:T(8,128)(2,1)}, bf16[12,112,256]{2,1,0:T(8...) custom-call(s32[8,6]{1,0:T(8,128)} %get-tuple-element.38.rows_ref, ...), custom_call_target="tpu_custom_call" | custom-call | tf_op jit(solution)/shard_map/pallas_call | solution.py:66
  392.3 2.7 collective-permute-start.3
  396.1 17.8 %shard_map.77 = bf16[8,24,16,128]{3,2,1,0:T(8,128)(2,1)} custom-call(s32[12,2]{1,0:T(8,128)} %copy-done.17, bf16[24,384,128]{2,1,0:T(8,128)(2,1)} %bitcast.1.w_ref, bf16[12,112,256]{2,1,0:T(8,128)(2,1)} %get-tuple-element.29.refs_0_, bf16[12,112,256]{2,1,0:T(8,128)(2,1)} %copy-done.8, bf16[12,112,256]{2,1,0:T(8,128)(2,1)} %copy-done.10, ...), custom_call_target="tpu_custom_call" | custom-call | flops 7046430720 | bytes 7077888 | tf_op jit(solution)/shard_map/pallas_call | solution.py:135
  413.9 6.9 %all-to-all-start.2 = ((bf16[8,24,16,128]{3,2,1,0:T(8,128)(2,1)}), bf16[8,24,16,128]{3,2,1,0:T(8,128)(2,1)S(1)}, u32[]{:S(2)}, u32[]{:S(2)}) async-start(bf16[8,24,16,128]{3,2,1,0:T(8,128)(2,1)} %shard_map.77), calls=%async_computation.2 | async-start | bytes 1572864 | tf_op jit(solution)/shard_map/all_to_all | solution.py:181
  420.8 2.0 collective-permute-start.6
  422.9 2.6 collective-permute-start.7
  425.5 1.6 collective-permute-start.1
  427.1 1.7 collective-permute-start.2
  428.9 28.0 %collective-permute-done.5.refs_3_ = bf16[12,112,256]{2,1,0:T(8,128)(2,1)S(1)} collective-permute-done((bf16[12,112,256]{2,1,0:T(8,128)(2,1)}, bf16[12,112,256]{2,1,0:T(8,128)(2,1)S(1)}, u32[]{:S(2)}, u32[]{:S(2)}) %collective-permute-start.5) | collective-permute-done | bytes 688160 | tf_op jit(solution)/shard_map/ppermute | solution.py:172
  456.8 1.9 collective-permute-done.6.refs_4_
  458.7 0.8 copy-done.15
  459.6 0.8 copy-done.16
  460.4 13.9 %shard_map.74.refs_2_ = f32[24,128,128]{2,1,0:T(8,128)} custom-call(s32[12,2]{1,0:T(8,128)} %copy-done.2, bf16[24,384,128]{2,1,0:T(8,128)(2,1)} %bitcast.4, bf16[12,112,256]{2,1,0:T(8,128)(2,1)} %get-tuple-element.23.refs_0_, bf16[12,112,256]{2,1,0:T(8,128)(2,1)} %collective-permute-done.3.refs_1_, bf16[12,112,256]{2,1,0:T(8,128)(2,1)} %collective-permute-done.4.refs_2_, ...), custom_call_target="tpu_custom_call" | custom-call | flops 5284823040 | bytes 5701632 | tf_op jit(solution)/shard_map/pallas_call | solution.py:135
  474.3 13.5 %shard_map.75 = bf16[8,24,16,128]{3,2,1,0:T(8,128)(2,1)} custom-call(s32[12,2]{1,0:T(8,128)} %copy-done.2, bf16[24,384,128]{2,1,0:T(8,128)(2,1)} %bitcast.5, bf16[12,112,256]{2,1,0:T(8,128)(2,1)} %collective-permute-done.1.refs_0_, bf16[12,112,256]{2,1,0:T(8,128)(2,1)} %collective-permute-done.2.refs_1_, f32[24,128,128]{2,1,0:T(8,128)} %shard_map.74.refs_2_), custom_call_target="tpu_custom_call" | custom-call | flops 1761607680 | bytes 2949120 | tf_op jit(solution)/shard_map/pallas_call | solution.py:135
  487.9 6.9 %all-to-all-start = ((bf16[8,24,16,128]{3,2,1,0:T(8,128)(2,1)}), bf16[8,24,16,128]{3,2,1,0:T(8,128)(2,1)S(1)}, u32[]{:S(2)}, u32[]{:S(2)}) async-start(bf16[8,24,16,128]{3,2,1,0:T(8,128)(2,1)} %shard_map.75), calls=%async_computation | async-start | bytes 1572864 | tf_op jit(solution)/shard_map/all_to_all | solution.py:181
  494.9 2.9 collective-permute-start.17
  497.8 12.1 %all-to-all-done = bf16[8,24,16,128]{3,2,1,0:T(8,128)(2,1)S(1)} async-done(((bf16[8,24,16,128]{3,2,1,0:T(8,128)(2,1)}), bf16[8,24,16,128]{3,2,1,0:T(8,128)(2,1)S(1)}, u32[]{:S(2)}, u32[]{:S(2)}) %all-to-all-start) | async-done | bytes 786464 | tf_op jit(solution)/shard_map/all_to_all | solution.py:181
  (68 shorter events, 4.5 us)
Async XLA Ops:
  0.0 28.9 %collective-permute-start = (bf16[64,112,256]{2,1,0:T(8,128)(2,1)}, bf16[64,112,256]{2,1,0:T(8,128)(2,1)}, u32[]{:S(2)}, u32[]{:S(2)}) collective-permute-start(bf16[64,112,256]{2,1,0:T(8,128)(2,1)} %panels_ref.3), channel_id=1, source_target_pairs={{0,8},{8,0},{16,24},{24,16},{32,40},{40,32},{48,56},{56,48},{64,72... | collective-permute-start | bytes 11010056 | tf_op jit(solution)/shard_map/ppermute | solution.py:150
  3.0 15.3 %copy-start = (bf16[12,2,384,128]{3,2,1,0:T(8,128)(2,1)}, bf16[12,2,384,128]{3,2,1,0:T(8,128)(2,1)S(1)}, u32[]{:S(2)}) copy-start(bf16[12,2,384,128]{3,2,1,0:T(8,128)(2,1)S(1)} %pad_maximum_fusion) | copy-start | bytes 7077892
  3.0 13.3 %collective-permute-start.9 = (bf16[3,384,128]{2,1,0:T(8,128)(2,1)S(1)}, bf16[3,384,128]{2,1,0:T(8,128)(2,1)S(1)}, u32[]{:S(2)}, u32[]{:S(2)}) collective-permute-start(bf16[3,384,128]{2,1,0:T(8,128)(2,1)S(1)} %constant_dynamic-slice_fusion), channel_id=1, source_target_pairs={{0,160},{8,168},{16,176},{24,184},{32,128},{40,136},{48,144},{56,1... | collective-permute-start | bytes 884744 | tf_op jit(solution)/shard_map/ppermute | solution.py:160
  18.3 8.6 %copy-start.3 = (s32[32,6]{0,1:T(8,128)S(1)}, s32[32,6]{0,1:T(8,128)}, u32[]{:S(2)}) copy-start(s32[32,6]{0,1:T(8,128)} %param.8) | copy-start | bytes 2308
  18.3 376.8 %all-to-all-start.1 = ((bf16[8,3,384,128]{3,2,1,0:T(8,128)(2,1)}), bf16[8,3,384,128]{3,2,1,0:T(8,128)(2,1)}, u32[]{:S(2)}, u32[]{:S(2)}) async-start(bf16[8,3,384,128]{3,2,1,0:T(8,128)(2,1)} %broadcast_in_dim.32), calls=%async_computation.1 | async-start | bytes 4718592 | tf_op jit(solution)/shard_map/all_to_all | solution.py:161
  28.9 171.7 %copy-start.4 = (s32[12,2]{0,1:T(2,128)S(1)}, s32[12,2]{0,1:T(2,128)}, u32[]{:S(2)}) copy-start(s32[12,2]{0,1:T(2,128)} %param.9) | copy-start | bytes 292
  198.5 22.1 %collective-permute-start.10 = (bf16[12,112,256]{2,1,0:T(8,128)(2,1)}, bf16[12,112,256]{2,1,0:T(8,128)(2,1)S(1)}, u32[]{:S(2)}, u32[]{:S(2)}) collective-permute-start(bf16[12,112,256]{2,1,0:T(8,128)(2,1)} %get-tuple-element.30), channel_id=1, source_target_pairs={{0,64},{8,72},{16,80},{24,88},{32,96},{40,104},{48,112},{56,120},{... | collective-permute-start | bytes 2064392 | tf_op jit(solution)/shard_map/ppermute | solution.py:172
  199.8 21.8 %collective-permute-start.11 = (bf16[12,112,256]{2,1,0:T(8,128)(2,1)}, bf16[12,112,256]{2,1,0:T(8,128)(2,1)S(1)}, u32[]{:S(2)}, u32[]{:S(2)}) collective-permute-start(bf16[12,112,256]{2,1,0:T(8,128)(2,1)} %get-tuple-element.31), channel_id=1, source_target_pairs={{0,192},{8,200},{16,208},{24,216},{32,224},{40,232},{48,240},{56,2... | collective-permute-start | bytes 2064392 | tf_op jit(solution)/shard_map/ppermute | solution.py:172
  200.7 191.5 %copy-start.2 = (s32[12,2]{1,0:T(8,128)}, s32[12,2]{1,0:T(8,128)S(1)}, u32[]{:S(2)}) copy-start(s32[12,2]{1,0:T(8,128)S(1)} %copy.11.slots_ref) | copy-start | bytes 292
  200.7 16.7 %collective-permute-start.8 = (s32[12,2]{1,0:T(8,128)S(1)}, s32[12,2]{1,0:T(8,128)S(1)}, u32[]{:S(2)}, u32[]{:S(2)}) collective-permute-start(s32[12,2]{1,0:T(8,128)S(1)} %copy.11.slots_ref), channel_id=1, source_target_pairs={{0,160},{8,168},{16,176},{24,184},{32,128},{40,136},{48,144},{56,1... | collective-permute-start | bytes 296 | tf_op jit(solution)/shard_map/ppermute | solution.py:149
  204.2 188.1 %collective-permute-start.12 = (bf16[12,112,256]{2,1,0:T(8,128)(2,1)}, bf16[12,112,256]{2,1,0:T(8,128)(2,1)S(1)}, u32[]{:S(2)}, u32[]{:S(2)}) collective-permute-start(bf16[12,112,256]{2,1,0:T(8,128)(2,1)} %get-tuple-element.32), channel_id=1, source_target_pairs={{0,16},{8,24},{16,32},{24,40},{32,48},{40,56},{48,0},{56,8},{64,80... | collective-permute-start | bytes 2064392 | tf_op jit(solution)/shard_map/ppermute | solution.py:172
  204.2 190.8 %collective-permute-start.13 = (bf16[12,112,256]{2,1,0:T(8,128)(2,1)}, bf16[12,112,256]{2,1,0:T(8,128)(2,1)S(1)}, u32[]{:S(2)}, u32[]{:S(2)}) collective-permute-start(bf16[12,112,256]{2,1,0:T(8,128)(2,1)} %get-tuple-element.33), channel_id=1, source_target_pairs={{0,48},{8,56},{16,0},{24,8},{32,16},{40,24},{48,32},{56,40},{64,11... | collective-permute-start | bytes 2064392 | tf_op jit(solution)/shard_map/ppermute | solution.py:172
  217.4 174.8 %copy-start.17 = (s32[12,2]{1,0:T(8,128)}, s32[12,2]{1,0:T(8,128)S(1)}, u32[]{:S(2)}) copy-start(s32[12,2]{1,0:T(8,128)S(1)} %collective-permute-done.8.slots_ref) | copy-start | bytes 292
  217.4 177.6 %collective-permute-start.14 = (bf16[12,112,256]{2,1,0:T(8,128)(2,1)}, bf16[12,112,256]{2,1,0:T(8,128)(2,1)S(1)}, u32[]{:S(2)}, u32[]{:S(2)}) collective-permute-start(bf16[12,112,256]{2,1,0:T(8,128)(2,1)} %get-tuple-element.34), channel_id=1, source_target_pairs={{0,240},{8,88},{16,192},{24,104},{32,208},{40,120},{48,224},{56,72... | collective-permute-start | bytes 2064392 | tf_op jit(solution)/shard_map/ppermute | solution.py:172
  220.6 171.7 %copy-start.8 = (bf16[12,112,256]{2,1,0:T(8,128)(2,1)}, bf16[12,112,256]{2,1,0:T(8,128)(2,1)S(1)}, u32[]{:S(2)}) copy-start(bf16[12,112,256]{2,1,0:T(8,128)(2,1)S(1)} %collective-permute-done.10.refs_1_) | copy-start | bytes 2064388
  220.6 174.4 %collective-permute-start.15 = (bf16[12,112,256]{2,1,0:T(8,128)(2,1)}, bf16[12,112,256]{2,1,0:T(8,128)(2,1)}, u32[]{:S(2)}, u32[]{:S(2)}) collective-permute-start(bf16[12,112,256]{2,1,0:T(8,128)(2,1)} %get-tuple-element.35), channel_id=1, source_target_pairs={{0,208},{8,120},{16,224},{24,72},{32,240},{40,88},{48,192},{56,104... | collective-permute-start | bytes 2064392 | tf_op jit(solution)/shard_map/ppermute | solution.py:172
  221.6 170.7 %copy-start.10 = (bf16[12,112,256]{2,1,0:T(8,128)(2,1)}, bf16[12,112,256]{2,1,0:T(8,128)(2,1)S(1)}, u32[]{:S(2)}) copy-start(bf16[12,112,256]{2,1,0:T(8,128)(2,1)S(1)} %collective-permute-done.11.refs_2_) | copy-start | bytes 2064388
  221.6 173.4 %collective-permute-start.16 = (bf16[12,112,256]{2,1,0:T(8,128)(2,1)}, bf16[12,112,256]{2,1,0:T(8,128)(2,1)}, u32[]{:S(2)}, u32[]{:S(2)}) collective-permute-start(bf16[12,112,256]{2,1,0:T(8,128)(2,1)} %get-tuple-element.36), channel_id=1, source_target_pairs={{0,128},{8,40},{16,144},{24,56},{32,160},{40,8},{48,176},{56,24},{... | collective-permute-start | bytes 2064392 | tf_op jit(solution)/shard_map/ppermute | solution.py:172
  392.3 33.2 %collective-permute-start.3 = (bf16[12,112,256]{2,1,0:T(8,128)(2,1)}, bf16[12,112,256]{2,1,0:T(8,128)(2,1)}, u32[]{:S(2)}, u32[]{:S(2)}) collective-permute-start(bf16[12,112,256]{2,1,0:T(8,128)(2,1)} %get-tuple-element.24), channel_id=1, source_target_pairs={{0,64},{8,72},{16,80},{24,88},{32,96},{40,104},{48,112},{56,120},{... | collective-permute-start | bytes 2064392 | tf_op jit(solution)/shard_map/ppermute | solution.py:172
  395.0 32.2 %collective-permute-start.4 = (bf16[12,112,256]{2,1,0:T(8,128)(2,1)}, bf16[12,112,256]{2,1,0:T(8,128)(2,1)}, u32[]{:S(2)}, u32[]{:S(2)}) collective-permute-start(bf16[12,112,256]{2,1,0:T(8,128)(2,1)} %get-tuple-element.25), channel_id=1, source_target_pairs={{0,192},{8,200},{16,208},{24,216},{32,224},{40,232},{48,240},{56,2... | collective-permute-start | bytes 2064392 | tf_op jit(solution)/shard_map/ppermute | solution.py:172
  396.1 24.8 %copy-start.9 = (bf16[12,112,256]{2,1,0:T(8,128)(2,1)S(1)}, bf16[12,112,256]{2,1,0:T(8,128)(2,1)}, u32[]{:S(2)}) copy-start(bf16[12,112,256]{2,1,0:T(8,128)(2,1)} %get-tuple-element.27) | copy-start | bytes 2064388
  396.1 26.8 %copy-start.7 = (bf16[12,112,256]{2,1,0:T(8,128)(2,1)S(1)}, bf16[12,112,256]{2,1,0:T(8,128)(2,1)}, u32[]{:S(2)}) copy-start(bf16[12,112,256]{2,1,0:T(8,128)(2,1)} %get-tuple-element.28) | copy-start | bytes 2064388
  396.1 29.5 %copy-start.6 = (bf16[12,112,256]{2,1,0:T(8,128)(2,1)S(1)}, bf16[12,112,256]{2,1,0:T(8,128)(2,1)}, u32[]{:S(2)}) copy-start(bf16[12,112,256]{2,1,0:T(8,128)(2,1)} %get-tuple-element.21) | copy-start | bytes 2064388
  396.1 31.1 %copy-start.5 = (bf16[12,112,256]{2,1,0:T(8,128)(2,1)S(1)}, bf16[12,112,256]{2,1,0:T(8,128)(2,1)}, u32[]{:S(2)}) copy-start(bf16[12,112,256]{2,1,0:T(8,128)(2,1)} %get-tuple-element.22) | copy-start | bytes 2064388
  413.9 74.0 %all-to-all-start.2 = ((bf16[8,24,16,128]{3,2,1,0:T(8,128)(2,1)}), bf16[8,24,16,128]{3,2,1,0:T(8,128)(2,1)S(1)}, u32[]{:S(2)}, u32[]{:S(2)}) async-start(bf16[8,24,16,128]{3,2,1,0:T(8,128)(2,1)} %shard_map.77), calls=%async_computation.2 | async-start | bytes 1572864 | tf_op jit(solution)/shard_map/all_to_all | solution.py:181
  420.8 36.0 %collective-permute-start.5 = (bf16[12,112,256]{2,1,0:T(8,128)(2,1)}, bf16[12,112,256]{2,1,0:T(8,128)(2,1)S(1)}, u32[]{:S(2)}, u32[]{:S(2)}) collective-permute-start(bf16[12,112,256]{2,1,0:T(8,128)(2,1)} %get-tuple-element.26), channel_id=1, source_target_pairs={{0,16},{8,24},{16,32},{24,40},{32,48},{40,56},{48,0},{56,8},{64,80... | collective-permute-start | bytes 2064392 | tf_op jit(solution)/shard_map/ppermute | solution.py:172
  420.8 37.9 %collective-permute-start.6 = (bf16[12,112,256]{2,1,0:T(8,128)(2,1)S(1)}, bf16[12,112,256]{2,1,0:T(8,128)(2,1)S(1)}, u32[]{:S(2)}, u32[]{:S(2)}) collective-permute-start(bf16[12,112,256]{2,1,0:T(8,128)(2,1)S(1)} %copy-done.9), channel_id=1, source_target_pairs={{0,48},{8,56},{16,0},{24,8},{32,16},{40,24},{48,32},{56,40},{64,11... | collective-permute-start | bytes 2064392 | tf_op jit(solution)/shard_map/ppermute | solution.py:172
  422.9 35.9 %collective-permute-start.7 = (bf16[12,112,256]{2,1,0:T(8,128)(2,1)S(1)}, bf16[12,112,256]{2,1,0:T(8,128)(2,1)S(1)}, u32[]{:S(2)}, u32[]{:S(2)}) collective-permute-start(bf16[12,112,256]{2,1,0:T(8,128)(2,1)S(1)} %copy-done.7), channel_id=1, source_target_pairs={{0,240},{8,88},{16,192},{24,104},{32,208},{40,120},{48,224},{56,72... | collective-permute-start | bytes 2064392 | tf_op jit(solution)/shard_map/ppermute | solution.py:172
  425.5 48.8 %collective-permute-start.1 = (bf16[12,112,256]{2,1,0:T(8,128)(2,1)S(1)}, bf16[12,112,256]{2,1,0:T(8,128)(2,1)}, u32[]{:S(2)}, u32[]{:S(2)}) collective-permute-start(bf16[12,112,256]{2,1,0:T(8,128)(2,1)S(1)} %copy-done.6), channel_id=1, source_target_pairs={{0,208},{8,120},{16,224},{24,72},{32,240},{40,88},{48,192},{56,104... | collective-permute-start | bytes 2064392 | tf_op jit(solution)/shard_map/ppermute | solution.py:172
  427.1 47.2 %collective-permute-start.2 = (bf16[12,112,256]{2,1,0:T(8,128)(2,1)S(1)}, bf16[12,112,256]{2,1,0:T(8,128)(2,1)}, u32[]{:S(2)}, u32[]{:S(2)}) collective-permute-start(bf16[12,112,256]{2,1,0:T(8,128)(2,1)S(1)} %copy-done.5), channel_id=1, source_target_pairs={{0,128},{8,40},{16,144},{24,56},{32,160},{40,8},{48,176},{56,24},{... | collective-permute-start | bytes 2064392 | tf_op jit(solution)/shard_map/ppermute | solution.py:172
  487.9 22.0 %all-to-all-start = ((bf16[8,24,16,128]{3,2,1,0:T(8,128)(2,1)}), bf16[8,24,16,128]{3,2,1,0:T(8,128)(2,1)S(1)}, u32[]{:S(2)}, u32[]{:S(2)}) async-start(bf16[8,24,16,128]{3,2,1,0:T(8,128)(2,1)} %shard_map.75), calls=%async_computation | async-start | bytes 1572864 | tf_op jit(solution)/shard_map/all_to_all | solution.py:181
  494.9 15.1 %collective-permute-start.17 = (f32[24,16,128]{2,1,0:T(8,128)S(1)}, f32[24,16,128]{2,1,0:T(8,128)S(1)}, u32[]{:S(2)}, u32[]{:S(2)}) collective-permute-start(f32[24,16,128]{2,1,0:T(8,128)S(1)} %convert_reduce_fusion), channel_id=1, source_target_pairs={{0,160},{8,168},{16,176},{24,184},{32,128},{40,136},{48,144},{56,1... | collective-permute-start | bytes 589832 | tf_op jit(solution)/shard_map/ppermute | solution.py:184
  (7 other events, 10.9 us)
where the time goes:
time: 513 us; the launch traced here: 511 us
  Pallas kernels  384 us (75%)
  waiting for transfers between devices  64.1 us (12%)
  starting transfers between devices  51.3 us (10%)
  local copies, waits for them, and re-layouts  7.69 us (1%)
    pallas_call x2, Pallas kernels, collect(): pl.pallas_call(collect_kernel, out_shape=[block] * steps, in_specs=[pl.Bl...  339 us
    pallas_call x3, Pallas kernels, accumulate(): pl.pallas_call(functools.partial(kernel, count, first, last, pieces), out...  45.3 us
    ppermute x14, waiting for transfers between devices, per_device(): row.append(lax.ppermute(blocks[step], 'pairs', perms[step]))  29.9 us
    ppermute x14, starting transfers between devices, per_device(): row.append(lax.ppermute(blocks[step], 'pairs', perms[step]))  20.2 us
    all_to_all x2, starting transfers between devices, sums(): got = lax.all_to_all(total, 'aux', split_axis=0, concat_axis=0, tiled=True)  13.9 us
    all_to_all x2, waiting for transfers between devices, sums(): got = lax.all_to_all(total, 'aux', split_axis=0, concat_axis=0, tiled=True)  12.1 us
    ppermute x1, waiting for transfers between devices, per_device(): partner_slots = lax.ppermute(pair_slots, 'pairs', partner)  11.2 us
    ppermute x1, waiting for transfers between devices, per_device(): lax.ppermute(lax.dynamic_slice_in_dim(own_w, z * share, share, 0), 'pairs...  11 us
  transfers between devices with their start and end apart: 21, of which 5 were waited for; matrix products, arithmetic and copies ran while one was open for 1% of the time, Pallas kernels for 75%

commit v1 on v0

--- a/solution.py
+++ b/solution.py
@@ -10,6 +10,7 @@
 
 
 SIDE = 4
+TOGETHER = 3
 BATCHES = ((8,), (6, 2))
 
 STEPS = (
@@ -39,36 +40,24 @@
     return perms, np.asarray(targets, np.int32).transpose(1, 2, 0)
 
 
-def collect_kernel(rows_ref, panels_ref, sibling_ref, *refs):
-    outs, sems = refs[:-1], refs[-1]
+def collect_kernel(rows_ref, panels_ref, sibling_ref, *outs):
     slots = rows_ref.shape[1]
-    copies = []
     for step, out_ref in enumerate(outs):
         for slot in range(slots):
-            for half, source_ref in enumerate((panels_ref, sibling_ref)):
-                copies.append(
-                    pltpu.make_async_copy(
-                        source_ref.at[rows_ref[step, slot]],
-                        out_ref.at[half * slots + slot],
-                        sems.at[(step * slots + slot) * 2 + half],
-                    )
-                )
-    for copy in copies:
-        copy.start()
-    for copy in copies:
-        copy.wait()
+            row = rows_ref[step, slot]
+            out_ref[slot] = panels_ref[row]
+            out_ref[slots + slot] = sibling_ref[row]
 
 
 def collect(rows, panels, sibling):
     steps, slots = rows.shape
-    anywhere = pl.BlockSpec(memory_space=pl.ANY)
+    vmem = pl.BlockSpec(memory_space=pltpu.VMEM)
     block = jax.ShapeDtypeStruct((2 * slots,) + panels.shape[1:], panels.dtype)
     return pl.pallas_call(
         collect_kernel,
         out_shape=[block] * steps,
-        in_specs=[pl.BlockSpec(memory_space=pltpu.SMEM), anywhere, anywhere],
-        out_specs=[anywhere] * steps,
-        scratch_shapes=[pltpu.SemaphoreType.DMA((steps * slots * 2,))],
+        in_specs=[pl.BlockSpec(memory_space=pltpu.SMEM), vmem, vmem],
+        out_specs=[vmem] * steps,
     )(rows, panels, sibling)
 
 
@@ -101,26 +90,33 @@
 
     slots = blocks[0].shape[0] // 2
 
-    def pair(p, carry):
+    def partial_of(p):
         i, j = slots_ref[p, 0], slots_ref[p, 1]
         coeffs = jnp.concatenate([w_ref[2 * p, :v, :], w_ref[2 * p + 1, :v, :]], axis=1)
         lefts = [b[half * slots + i] for b in blocks for half in range(2)]
         rights = [b[half * slots + j] for b in blocks for half in range(2)]
         total = contribution(lefts, rights, coeffs)
-        for root in range(2):
-            k = total[root]
-            if not first:
-                k = k + refs[count][2 * p + root]
-            if last:
-                sigma = dress(k, w_ref[2 * p + root, v:, :]).astype(jnp.bfloat16)
-                rows = sigma.shape[0] // pieces
-                for piece in range(pieces):
-                    out_ref[piece, 2 * p + root] = sigma[piece * rows : (piece + 1) * rows]
-            else:
-                out_ref[2 * p + root] = k
+        if not first:
+            total = [k + refs[count][2 * p + root] for root, k in enumerate(total)]
+        return total
+
+    def store(at, k):
+        if not last:
+            out_ref[at] = k
+            return
+        sigma = dress(k, w_ref[at, v:, :]).astype(jnp.bfloat16)
+        rows = sigma.shape[0] // pieces
+        for piece in range(pieces):
+            out_ref[piece, at] = sigma[piece * rows : (piece + 1) * rows]
+
+    def pairs(step, carry):
+        totals = [partial_of(step * TOGETHER + n) for n in range(TOGETHER)]
+        for n, total in enumerate(totals):
+            for root, k in enumerate(total):
+                store(2 * (step * TOGETHER + n) + root, k)
         return carry
 
-    lax.fori_loop(0, slots_ref.shape[0], pair, 0)
+    lax.fori_loop(0, slots_ref.shape[0] // TOGETHER, pairs, 0)
 
 
 def accumulate(slots, w, blocks, total, last, pieces):

time: 513 us -> 195 us (0.38)
  Pallas kernels: 384 us -> 48.8 us
  waiting for transfers between devices: 64.1 us -> 80.2 us
    pallas_call x2, Pallas kernels: 339 us -> 11.7 us  [collect(): pl.pallas_call(collect_kernel, out_shape=[block] * steps, in_specs=[pl.Bl...]
    ppermute x14, waiting for transfers between devices: 29.9 us -> 45.6 us  [per_device(): row.append(lax.ppermute(blocks[step], 'pairs', perms[step]))]
    pallas_call x3, Pallas kernels: 45.3 us -> 37.1 us  [accumulate(): pl.pallas_call(functools.partial(kernel, count, first, last, pieces), out...]
  transfers between devices with their start and end apart: 21 -> 21, of which waited for: 5 -> 7; matrix products, arithmetic and copies ran while one was open for 1% -> 4% of each run, Pallas kernels for 75% -> 25%
where the time goes in v1:
time: 195 us; the launch traced here: 192 us
  waiting for transfers between devices  80.2 us (41%)
  starting transfers between devices  53.2 us (27%)
  Pallas kernels  48.8 us (25%)
  local copies, waits for them, and re-layouts  6.7 us (3%)
  other arithmetic  2.89 us (1%)
    ppermute x14, waiting for transfers between devices, per_device(): row.append(lax.ppermute(blocks[step], 'pairs', perms[step]))  45.6 us
    pallas_call x3, Pallas kernels, accumulate(): pl.pallas_call(functools.partial(kernel, count, first, last, pieces), out...  37.1 us
    ppermute x14, starting transfers between devices, per_device(): row.append(lax.ppermute(blocks[step], 'pairs', perms[step]))  20.5 us
    all_to_all x2, starting transfers between devices, sums(): got = lax.all_to_all(total, 'aux', split_axis=0, concat_axis=0, tiled=True)  14.8 us
    all_to_all x2, waiting for transfers between devices, sums(): got = lax.all_to_all(total, 'aux', split_axis=0, concat_axis=0, tiled=True)  12.5 us
    pallas_call x2, Pallas kernels, collect(): pl.pallas_call(collect_kernel, out_shape=[block] * steps, in_specs=[pl.Bl...  11.7 us
    ppermute x1, waiting for transfers between devices, per_device(): partner_slots = lax.ppermute(pair_slots, 'pairs', partner)  11.2 us
    ppermute x1, waiting for transfers between devices, per_device(): lax.ppermute(lax.dynamic_slice_in_dim(own_w, z * share, share, 0), 'pairs...  11 us
  transfers between devices with their start and end apart: 21, of which 7 were waited for; matrix products, arithmetic and copies ran while one was open for 4% of the time, Pallas kernels for 25%

profile of v1, /device:TPU:12, one launch (start us, length us, event | category | flops | bytes accessed | tf_op | source)
XLA Modules:
  0.0 192.1 jit_solution(15628221528095641121)
XLA Ops:
  0.0 0.9 copy.8
  1.0 1.6 and_select_fusion
  3.0 2.3 %collective-permute-start.9 = (bf16[3,384,128]{2,1,0:T(8,128)(2,1)S(1)}, bf16[3,384,128]{2,1,0:T(8,128)(2,1)S(1)}, u32[]{:S(2)}, u32[]{:S(2)}) collective-permute-start(bf16[3,384,128]{2,1,0:T(8,128)(2,1)S(1)} %constant_dynamic-slice_fusion), channel_id=1, source_target_pairs={{0,160},{8,168},{16,176},{24,184},{32,128},{40,136},{48,144},{56,1... | collective-permute-start | bytes 884744 | tf_op jit(solution)/shard_map/ppermute | solution.py:156
  5.3 11.0 %collective-permute-done.9 = bf16[3,384,128]{2,1,0:T(8,128)(2,1)S(1)} collective-permute-done((bf16[3,384,128]{2,1,0:T(8,128)(2,1)S(1)}, bf16[3,384,128]{2,1,0:T(8,128)(2,1)S(1)}, u32[]{:S(2)}, u32[]{:S(2)}) %collective-permute-start.9) | collective-permute-done | bytes 294944 | tf_op jit(solution)/shard_map/ppermute | solution.py:156
  16.3 2.0 %broadcast_in_dim.32 = bf16[8,3,384,128]{3,2,1,0:T(8,128)(2,1)} broadcast(bf16[3,384,128]{2,1,0:T(8,128)(2,1)S(1)} %collective-permute-done.9), dimensions={1,2,3} | broadcast | bytes 2654208 | tf_op jit(solution)/shard_map/broadcast_in_dim | solution.py:158
  18.3 8.6 %all-to-all-start.1 = ((bf16[8,3,384,128]{3,2,1,0:T(8,128)(2,1)}), bf16[8,3,384,128]{3,2,1,0:T(8,128)(2,1)}, u32[]{:S(2)}, u32[]{:S(2)}) async-start(bf16[8,3,384,128]{3,2,1,0:T(8,128)(2,1)} %broadcast_in_dim.32), calls=%async_computation.1 | async-start | bytes 4718592 | tf_op jit(solution)/shard_map/all_to_all | solution.py:157
  28.9 5.9 %shard_map.76 = (bf16[12,112,256]{2,1,0:T(8,128)(2,1)}, bf16[12,112,256]{2,1,0:T(8,128)(2,1)}, bf16[12,112,256]{2,1,0:T(8,128)(2,1)}, bf16[12,112,256]{2,1,0:T(8...) custom-call(s32[8,6]{1,0:T(8,128)} %get-tuple-element.37.rows_ref, ...), custom_call_target="tpu_custom_call" | custom-call | tf_op jit(solution)/shard_map/pallas_call | solution.py:56
  34.8 1.2 collective-permute-start.10
  36.0 0.8 collective-permute-start.11
  36.9 3.5 %collective-permute-start.8 = (s32[12,2]{1,0:T(8,128)S(1)}, s32[12,2]{1,0:T(8,128)S(1)}, u32[]{:S(2)}, u32[]{:S(2)}) collective-permute-start(s32[12,2]{1,0:T(8,128)S(1)} %copy.11.slots_ref), channel_id=1, source_target_pairs={{0,160},{8,168},{16,176},{24,184},{32,128},{40,136},{48,144},{56,1... | collective-permute-start | bytes 296 | tf_op jit(solution)/shard_map/ppermute | solution.py:145
  40.4 2.0 %collective-permute-start.13 = (bf16[12,112,256]{2,1,0:T(8,128)(2,1)}, bf16[12,112,256]{2,1,0:T(8,128)(2,1)S(1)}, u32[]{:S(2)}, u32[]{:S(2)}) collective-permute-start(bf16[12,112,256]{2,1,0:T(8,128)(2,1)} %get-tuple-element.33), channel_id=1, source_target_pairs={{0,48},{8,56},{16,0},{24,8},{32,16},{40,24},{48,32},{56,40},{64,11... | collective-permute-start | bytes 2064392 | tf_op jit(solution)/shard_map/ppermute | solution.py:168
  42.4 11.2 %collective-permute-done.8.slots_ref = s32[12,2]{1,0:T(8,128)S(1)} collective-permute-done((s32[12,2]{1,0:T(8,128)S(1)}, s32[12,2]{1,0:T(8,128)S(1)}, u32[]{:S(2)}, u32[]{:S(2)}) %collective-permute-start.8) | collective-permute-done | bytes 128 | tf_op jit(solution)/shard_map/ppermute | solution.py:145
  53.5 3.2 %collective-permute-start.14 = (bf16[12,112,256]{2,1,0:T(8,128)(2,1)}, bf16[12,112,256]{2,1,0:T(8,128)(2,1)S(1)}, u32[]{:S(2)}, u32[]{:S(2)}) collective-permute-start(bf16[12,112,256]{2,1,0:T(8,128)(2,1)} %get-tuple-element.34), channel_id=1, source_target_pairs={{0,240},{8,88},{16,192},{24,104},{32,208},{40,120},{48,224},{56,72... | collective-permute-start | bytes 2064392 | tf_op jit(solution)/shard_map/ppermute | solution.py:168
  56.7 1.0 collective-permute-start.15
  57.8 1.1 collective-permute-start.16
  58.9 5.9 %shard_map.73 = (bf16[12,112,256]{2,1,0:T(8,128)(2,1)}, bf16[12,112,256]{2,1,0:T(8,128)(2,1)}, bf16[12,112,256]{2,1,0:T(8,128)(2,1)}, bf16[12,112,256]{2,1,0:T(8...) custom-call(s32[8,6]{1,0:T(8,128)} %get-tuple-element.38.rows_ref, ...), custom_call_target="tpu_custom_call" | custom-call | tf_op jit(solution)/shard_map/pallas_call | solution.py:56
  64.8 2.7 %collective-permute-start.3 = (bf16[12,112,256]{2,1,0:T(8,128)(2,1)}, bf16[12,112,256]{2,1,0:T(8,128)(2,1)}, u32[]{:S(2)}, u32[]{:S(2)}) collective-permute-start(bf16[12,112,256]{2,1,0:T(8,128)(2,1)} %get-tuple-element.24), channel_id=1, source_target_pairs={{0,64},{8,72},{16,80},{24,88},{32,96},{40,104},{48,112},{56,120},{... | collective-permute-start | bytes 2064392 | tf_op jit(solution)/shard_map/ppermute | solution.py:168
  67.5 1.0 collective-permute-done.14.refs_5_
  68.6 20.3 %collective-permute-done.15.refs_6_ = bf16[12,112,256]{2,1,0:T(8,128)(2,1)} collective-permute-done((bf16[12,112,256]{2,1,0:T(8,128)(2,1)}, bf16[12,112,256]{2,1,0:T(8,128)(2,1)}, u32[]{:S(2)}, u32[]{:S(2)}) %collective-permute-start.15) | collective-permute-done | bytes 688160 | tf_op jit(solution)/shard_map/ppermute | solution.py:168
  89.0 15.2 %shard_map.77 = bf16[8,24,16,128]{3,2,1,0:T(8,128)(2,1)} custom-call(s32[12,2]{1,0:T(8,128)} %copy-done.17, bf16[24,384,128]{2,1,0:T(8,128)(2,1)} %bitcast.1.w_ref, bf16[12,112,256]{2,1,0:T(8,128)(2,1)} %get-tuple-element.29.refs_0_, bf16[12,112,256]{2,1,0:T(8,128)(2,1)} %copy-done.8, bf16[12,112,256]{2,1,0:T(8,128)(2,1)} %copy-done.10, ...), custom_call_target="tpu_custom_call" | custom-call | flops 7046430720 | bytes 7077888 | tf_op jit(solution)/shard_map/pallas_call | solution.py:131
  104.2 7.1 %all-to-all-start.2 = ((bf16[8,24,16,128]{3,2,1,0:T(8,128)(2,1)}), bf16[8,24,16,128]{3,2,1,0:T(8,128)(2,1)S(1)}, u32[]{:S(2)}, u32[]{:S(2)}) async-start(bf16[8,24,16,128]{3,2,1,0:T(8,128)(2,1)} %shard_map.77), calls=%async_computation.2 | async-start | bytes 1572864 | tf_op jit(solution)/shard_map/all_to_all | solution.py:177
  111.3 2.0 %collective-permute-start.6 = (bf16[12,112,256]{2,1,0:T(8,128)(2,1)S(1)}, bf16[12,112,256]{2,1,0:T(8,128)(2,1)S(1)}, u32[]{:S(2)}, u32[]{:S(2)}) collective-permute-start(bf16[12,112,256]{2,1,0:T(8,128)(2,1)S(1)} %copy-done.9), channel_id=1, source_target_pairs={{0,48},{8,56},{16,0},{24,8},{32,16},{40,24},{48,32},{56,40},{64,11... | collective-permute-start | bytes 2064392 | tf_op jit(solution)/shard_map/ppermute | solution.py:168
  113.3 3.8 %collective-permute-start.7 = (bf16[12,112,256]{2,1,0:T(8,128)(2,1)S(1)}, bf16[12,112,256]{2,1,0:T(8,128)(2,1)S(1)}, u32[]{:S(2)}, u32[]{:S(2)}) collective-permute-start(bf16[12,112,256]{2,1,0:T(8,128)(2,1)S(1)} %copy-done.7), channel_id=1, source_target_pairs={{0,240},{8,88},{16,192},{24,104},{32,208},{40,120},{48,224},{56,72... | collective-permute-start | bytes 2064392 | tf_op jit(solution)/shard_map/ppermute | solution.py:168
  117.1 2.7 %collective-permute-start.2 = (bf16[12,112,256]{2,1,0:T(8,128)(2,1)S(1)}, bf16[12,112,256]{2,1,0:T(8,128)(2,1)}, u32[]{:S(2)}, u32[]{:S(2)}) collective-permute-start(bf16[12,112,256]{2,1,0:T(8,128)(2,1)S(1)} %copy-done.5), channel_id=1, source_target_pairs={{0,128},{8,40},{16,144},{24,56},{32,160},{40,8},{48,176},{56,24},{... | collective-permute-start | bytes 2064392 | tf_op jit(solution)/shard_map/ppermute | solution.py:168
  119.7 11.4 %collective-permute-done.5.refs_3_ = bf16[12,112,256]{2,1,0:T(8,128)(2,1)S(1)} collective-permute-done((bf16[12,112,256]{2,1,0:T(8,128)(2,1)}, bf16[12,112,256]{2,1,0:T(8,128)(2,1)S(1)}, u32[]{:S(2)}, u32[]{:S(2)}) %collective-permute-start.5) | collective-permute-done | bytes 688160 | tf_op jit(solution)/shard_map/ppermute | solution.py:168
  131.1 12.8 %collective-permute-done.6.refs_4_ = bf16[12,112,256]{2,1,0:T(8,128)(2,1)S(1)} collective-permute-done((bf16[12,112,256]{2,1,0:T(8,128)(2,1)S(1)}, bf16[12,112,256]{2,1,0:T(8,128)(2,1)S(1)}, u32[]{:S(2)}, u32[]{:S(2)}) %collective-permute-start.6) | collective-permute-done | bytes 688160 | tf_op jit(solution)/shard_map/ppermute | solution.py:168
  144.7 0.8 copy-done.16
  145.6 12.6 %shard_map.74.refs_2_ = f32[24,128,128]{2,1,0:T(8,128)} custom-call(s32[12,2]{1,0:T(8,128)} %copy-done.2, bf16[24,384,128]{2,1,0:T(8,128)(2,1)} %bitcast.4, bf16[12,112,256]{2,1,0:T(8,128)(2,1)} %get-tuple-element.23.refs_0_, bf16[12,112,256]{2,1,0:T(8,128)(2,1)} %collective-permute-done.3.refs_1_, bf16[12,112,256]{2,1,0:T(8,128)(2,1)} %collective-permute-done.4.refs_2_, ...), custom_call_target="tpu_custom_call" | custom-call | flops 5284823040 | bytes 5701632 | tf_op jit(solution)/shard_map/pallas_call | solution.py:131
  158.2 9.2 %shard_map.75 = bf16[8,24,16,128]{3,2,1,0:T(8,128)(2,1)} custom-call(s32[12,2]{1,0:T(8,128)} %copy-done.2, bf16[24,384,128]{2,1,0:T(8,128)(2,1)} %bitcast.5, bf16[12,112,256]{2,1,0:T(8,128)(2,1)} %collective-permute-done.1.refs_0_, bf16[12,112,256]{2,1,0:T(8,128)(2,1)} %collective-permute-done.2.refs_1_, f32[24,128,128]{2,1,0:T(8,128)} %shard_map.74.refs_2_), custom_call_target="tpu_custom_call" | custom-call | flops 1761607680 | bytes 2949120 | tf_op jit(solution)/shard_map/pallas_call | solution.py:131
  167.5 7.7 %all-to-all-start = ((bf16[8,24,16,128]{3,2,1,0:T(8,128)(2,1)}), bf16[8,24,16,128]{3,2,1,0:T(8,128)(2,1)S(1)}, u32[]{:S(2)}, u32[]{:S(2)}) async-start(bf16[8,24,16,128]{3,2,1,0:T(8,128)(2,1)} %shard_map.75), calls=%async_computation | async-start | bytes 1572864 | tf_op jit(solution)/shard_map/all_to_all | solution.py:177
  175.3 3.5 %collective-permute-start.17 = (f32[24,16,128]{2,1,0:T(8,128)S(1)}, f32[24,16,128]{2,1,0:T(8,128)S(1)}, u32[]{:S(2)}, u32[]{:S(2)}) collective-permute-start(f32[24,16,128]{2,1,0:T(8,128)S(1)} %convert_reduce_fusion), channel_id=1, source_target_pairs={{0,160},{8,168},{16,176},{24,184},{32,128},{40,136},{48,144},{56,1... | collective-permute-start | bytes 589832 | tf_op jit(solution)/shard_map/ppermute | solution.py:180
  178.8 12.5 %all-to-all-done = bf16[8,24,16,128]{3,2,1,0:T(8,128)(2,1)S(1)} async-done(((bf16[8,24,16,128]{3,2,1,0:T(8,128)(2,1)}), bf16[8,24,16,128]{3,2,1,0:T(8,128)(2,1)S(1)}, u32[]{:S(2)}, u32[]{:S(2)}) %all-to-all-start) | async-done | bytes 786464 | tf_op jit(solution)/shard_map/all_to_all | solution.py:177
  (68 shorter events, 4.4 us)
Async XLA Ops:
  0.0 28.9 %collective-permute-start = (bf16[64,112,256]{2,1,0:T(8,128)(2,1)}, bf16[64,112,256]{2,1,0:T(8,128)(2,1)}, u32[]{:S(2)}, u32[]{:S(2)}) collective-permute-start(bf16[64,112,256]{2,1,0:T(8,128)(2,1)} %panels_ref.3), channel_id=1, source_target_pairs={{0,8},{8,0},{16,24},{24,16},{32,40},{40,32},{48,56},{56,48},{64,72... | collective-permute-start | bytes 11010056 | tf_op jit(solution)/shard_map/ppermute | solution.py:146
  3.0 15.3 %copy-start = (bf16[12,2,384,128]{3,2,1,0:T(8,128)(2,1)}, bf16[12,2,384,128]{3,2,1,0:T(8,128)(2,1)S(1)}, u32[]{:S(2)}) copy-start(bf16[12,2,384,128]{3,2,1,0:T(8,128)(2,1)S(1)} %pad_maximum_fusion) | copy-start | bytes 7077892
  3.0 13.3 %collective-permute-start.9 = (bf16[3,384,128]{2,1,0:T(8,128)(2,1)S(1)}, bf16[3,384,128]{2,1,0:T(8,128)(2,1)S(1)}, u32[]{:S(2)}, u32[]{:S(2)}) collective-permute-start(bf16[3,384,128]{2,1,0:T(8,128)(2,1)S(1)} %constant_dynamic-slice_fusion), channel_id=1, source_target_pairs={{0,160},{8,168},{16,176},{24,184},{32,128},{40,136},{48,144},{56,1... | collective-permute-start | bytes 884744 | tf_op jit(solution)/shard_map/ppermute | solution.py:156
  18.3 70.7 %all-to-all-start.1 = ((bf16[8,3,384,128]{3,2,1,0:T(8,128)(2,1)}), bf16[8,3,384,128]{3,2,1,0:T(8,128)(2,1)}, u32[]{:S(2)}, u32[]{:S(2)}) async-start(bf16[8,3,384,128]{3,2,1,0:T(8,128)(2,1)} %broadcast_in_dim.32), calls=%async_computation.1 | async-start | bytes 4718592 | tf_op jit(solution)/shard_map/all_to_all | solution.py:157
  34.8 22.0 %collective-permute-start.10 = (bf16[12,112,256]{2,1,0:T(8,128)(2,1)}, bf16[12,112,256]{2,1,0:T(8,128)(2,1)S(1)}, u32[]{:S(2)}, u32[]{:S(2)}) collective-permute-start(bf16[12,112,256]{2,1,0:T(8,128)(2,1)} %get-tuple-element.30), channel_id=1, source_target_pairs={{0,64},{8,72},{16,80},{24,88},{32,96},{40,104},{48,112},{56,120},{... | collective-permute-start | bytes 2064392 | tf_op jit(solution)/shard_map/ppermute | solution.py:168
  36.0 21.8 %collective-permute-start.11 = (bf16[12,112,256]{2,1,0:T(8,128)(2,1)}, bf16[12,112,256]{2,1,0:T(8,128)(2,1)S(1)}, u32[]{:S(2)}, u32[]{:S(2)}) collective-permute-start(bf16[12,112,256]{2,1,0:T(8,128)(2,1)} %get-tuple-element.31), channel_id=1, source_target_pairs={{0,192},{8,200},{16,208},{24,216},{32,224},{40,232},{48,240},{56,2... | collective-permute-start | bytes 2064392 | tf_op jit(solution)/shard_map/ppermute | solution.py:168
  36.9 27.9 %copy-start.2 = (s32[12,2]{1,0:T(8,128)}, s32[12,2]{1,0:T(8,128)S(1)}, u32[]{:S(2)}) copy-start(s32[12,2]{1,0:T(8,128)S(1)} %copy.11.slots_ref) | copy-start | bytes 292
  36.9 16.7 %collective-permute-start.8 = (s32[12,2]{1,0:T(8,128)S(1)}, s32[12,2]{1,0:T(8,128)S(1)}, u32[]{:S(2)}, u32[]{:S(2)}) collective-permute-start(s32[12,2]{1,0:T(8,128)S(1)} %copy.11.slots_ref), channel_id=1, source_target_pairs={{0,160},{8,168},{16,176},{24,184},{32,128},{40,136},{48,144},{56,1... | collective-permute-start | bytes 296 | tf_op jit(solution)/shard_map/ppermute | solution.py:145
  40.4 24.4 %collective-permute-start.12 = (bf16[12,112,256]{2,1,0:T(8,128)(2,1)}, bf16[12,112,256]{2,1,0:T(8,128)(2,1)S(1)}, u32[]{:S(2)}, u32[]{:S(2)}) collective-permute-start(bf16[12,112,256]{2,1,0:T(8,128)(2,1)} %get-tuple-element.32), channel_id=1, source_target_pairs={{0,16},{8,24},{16,32},{24,40},{32,48},{40,56},{48,0},{56,8},{64,80... | collective-permute-start | bytes 2064392 | tf_op jit(solution)/shard_map/ppermute | solution.py:168
  40.4 27.2 %collective-permute-start.13 = (bf16[12,112,256]{2,1,0:T(8,128)(2,1)}, bf16[12,112,256]{2,1,0:T(8,128)(2,1)S(1)}, u32[]{:S(2)}, u32[]{:S(2)}) collective-permute-start(bf16[12,112,256]{2,1,0:T(8,128)(2,1)} %get-tuple-element.33), channel_id=1, source_target_pairs={{0,48},{8,56},{16,0},{24,8},{32,16},{40,24},{48,32},{56,40},{64,11... | collective-permute-start | bytes 2064392 | tf_op jit(solution)/shard_map/ppermute | solution.py:168
  53.5 11.2 %copy-start.17 = (s32[12,2]{1,0:T(8,128)}, s32[12,2]{1,0:T(8,128)S(1)}, u32[]{:S(2)}) copy-start(s32[12,2]{1,0:T(8,128)S(1)} %collective-permute-done.8.slots_ref) | copy-start | bytes 292
  53.5 15.0 %collective-permute-start.14 = (bf16[12,112,256]{2,1,0:T(8,128)(2,1)}, bf16[12,112,256]{2,1,0:T(8,128)(2,1)S(1)}, u32[]{:S(2)}, u32[]{:S(2)}) collective-permute-start(bf16[12,112,256]{2,1,0:T(8,128)(2,1)} %get-tuple-element.34), channel_id=1, source_target_pairs={{0,240},{8,88},{16,192},{24,104},{32,208},{40,120},{48,224},{56,72... | collective-permute-start | bytes 2064392 | tf_op jit(solution)/shard_map/ppermute | solution.py:168
  56.7 32.2 %collective-permute-start.15 = (bf16[12,112,256]{2,1,0:T(8,128)(2,1)}, bf16[12,112,256]{2,1,0:T(8,128)(2,1)}, u32[]{:S(2)}, u32[]{:S(2)}) collective-permute-start(bf16[12,112,256]{2,1,0:T(8,128)(2,1)} %get-tuple-element.35), channel_id=1, source_target_pairs={{0,208},{8,120},{16,224},{24,72},{32,240},{40,88},{48,192},{56,104... | collective-permute-start | bytes 2064392 | tf_op jit(solution)/shard_map/ppermute | solution.py:168
  57.8 31.2 %collective-permute-start.16 = (bf16[12,112,256]{2,1,0:T(8,128)(2,1)}, bf16[12,112,256]{2,1,0:T(8,128)(2,1)}, u32[]{:S(2)}, u32[]{:S(2)}) collective-permute-start(bf16[12,112,256]{2,1,0:T(8,128)(2,1)} %get-tuple-element.36), channel_id=1, source_target_pairs={{0,128},{8,40},{16,144},{24,56},{32,160},{40,8},{48,176},{56,24},{... | collective-permute-start | bytes 2064392 | tf_op jit(solution)/shard_map/ppermute | solution.py:168
  64.8 24.1 %copy-start.11 = (bf16[12,112,256]{2,1,0:T(8,128)(2,1)}, bf16[12,112,256]{2,1,0:T(8,128)(2,1)S(1)}, u32[]{:S(2)}) copy-start(bf16[12,112,256]{2,1,0:T(8,128)(2,1)S(1)} %collective-permute-done.12.refs_3_) | copy-start | bytes 2064388
  64.8 52.3 %collective-permute-start.3 = (bf16[12,112,256]{2,1,0:T(8,128)(2,1)}, bf16[12,112,256]{2,1,0:T(8,128)(2,1)}, u32[]{:S(2)}, u32[]{:S(2)}) collective-permute-start(bf16[12,112,256]{2,1,0:T(8,128)(2,1)} %get-tuple-element.24), channel_id=1, source_target_pairs={{0,64},{8,72},{16,80},{24,88},{32,96},{40,104},{48,112},{56,120},{... | collective-permute-start | bytes 2064392 | tf_op jit(solution)/shard_map/ppermute | solution.py:168
  67.5 21.4 %copy-start.12 = (bf16[12,112,256]{2,1,0:T(8,128)(2,1)}, bf16[12,112,256]{2,1,0:T(8,128)(2,1)S(1)}, u32[]{:S(2)}) copy-start(bf16[12,112,256]{2,1,0:T(8,128)(2,1)S(1)} %collective-permute-done.13.refs_4_) | copy-start | bytes 2064388
  67.5 49.6 %collective-permute-start.4 = (bf16[12,112,256]{2,1,0:T(8,128)(2,1)}, bf16[12,112,256]{2,1,0:T(8,128)(2,1)}, u32[]{:S(2)}, u32[]{:S(2)}) collective-permute-start(bf16[12,112,256]{2,1,0:T(8,128)(2,1)} %get-tuple-element.25), channel_id=1, source_target_pairs={{0,192},{8,200},{16,208},{24,216},{32,224},{40,232},{48,240},{56,2... | collective-permute-start | bytes 2064392 | tf_op jit(solution)/shard_map/ppermute | solution.py:168
  68.6 20.4 %copy-start.13 = (bf16[12,112,256]{2,1,0:T(8,128)(2,1)}, bf16[12,112,256]{2,1,0:T(8,128)(2,1)S(1)}, u32[]{:S(2)}) copy-start(bf16[12,112,256]{2,1,0:T(8,128)(2,1)S(1)} %collective-permute-done.14.refs_5_) | copy-start | bytes 2064388
  88.9 22.3 %copy-start.9 = (bf16[12,112,256]{2,1,0:T(8,128)(2,1)S(1)}, bf16[12,112,256]{2,1,0:T(8,128)(2,1)}, u32[]{:S(2)}) copy-start(bf16[12,112,256]{2,1,0:T(8,128)(2,1)} %get-tuple-element.27) | copy-start | bytes 2064388
  88.9 24.3 %copy-start.7 = (bf16[12,112,256]{2,1,0:T(8,128)(2,1)S(1)}, bf16[12,112,256]{2,1,0:T(8,128)(2,1)}, u32[]{:S(2)}) copy-start(bf16[12,112,256]{2,1,0:T(8,128)(2,1)} %get-tuple-element.28) | copy-start | bytes 2064388
  89.0 28.1 %copy-start.6 = (bf16[12,112,256]{2,1,0:T(8,128)(2,1)S(1)}, bf16[12,112,256]{2,1,0:T(8,128)(2,1)}, u32[]{:S(2)}) copy-start(bf16[12,112,256]{2,1,0:T(8,128)(2,1)} %get-tuple-element.21) | copy-start | bytes 2064388
  89.0 28.1 %copy-start.5 = (bf16[12,112,256]{2,1,0:T(8,128)(2,1)S(1)}, bf16[12,112,256]{2,1,0:T(8,128)(2,1)}, u32[]{:S(2)}) copy-start(bf16[12,112,256]{2,1,0:T(8,128)(2,1)} %get-tuple-element.22) | copy-start | bytes 2064388
  104.2 63.3 %all-to-all-start.2 = ((bf16[8,24,16,128]{3,2,1,0:T(8,128)(2,1)}), bf16[8,24,16,128]{3,2,1,0:T(8,128)(2,1)S(1)}, u32[]{:S(2)}, u32[]{:S(2)}) async-start(bf16[8,24,16,128]{3,2,1,0:T(8,128)(2,1)} %shard_map.77), calls=%async_computation.2 | async-start | bytes 1572864 | tf_op jit(solution)/shard_map/all_to_all | solution.py:177
  111.2 19.9 %collective-permute-start.5 = (bf16[12,112,256]{2,1,0:T(8,128)(2,1)}, bf16[12,112,256]{2,1,0:T(8,128)(2,1)S(1)}, u32[]{:S(2)}, u32[]{:S(2)}) collective-permute-start(bf16[12,112,256]{2,1,0:T(8,128)(2,1)} %get-tuple-element.26), channel_id=1, source_target_pairs={{0,16},{8,24},{16,32},{24,40},{32,48},{40,56},{48,0},{56,8},{64,80... | collective-permute-start | bytes 2064392 | tf_op jit(solution)/shard_map/ppermute | solution.py:168
  111.3 32.6 %collective-permute-start.6 = (bf16[12,112,256]{2,1,0:T(8,128)(2,1)S(1)}, bf16[12,112,256]{2,1,0:T(8,128)(2,1)S(1)}, u32[]{:S(2)}, u32[]{:S(2)}) collective-permute-start(bf16[12,112,256]{2,1,0:T(8,128)(2,1)S(1)} %copy-done.9), channel_id=1, source_target_pairs={{0,48},{8,56},{16,0},{24,8},{32,16},{40,24},{48,32},{56,40},{64,11... | collective-permute-start | bytes 2064392 | tf_op jit(solution)/shard_map/ppermute | solution.py:168
  113.3 30.6 %collective-permute-start.7 = (bf16[12,112,256]{2,1,0:T(8,128)(2,1)S(1)}, bf16[12,112,256]{2,1,0:T(8,128)(2,1)S(1)}, u32[]{:S(2)}, u32[]{:S(2)}) collective-permute-start(bf16[12,112,256]{2,1,0:T(8,128)(2,1)S(1)} %copy-done.7), channel_id=1, source_target_pairs={{0,240},{8,88},{16,192},{24,104},{32,208},{40,120},{48,224},{56,72... | collective-permute-start | bytes 2064392 | tf_op jit(solution)/shard_map/ppermute | solution.py:168
  117.1 41.2 %collective-permute-start.1 = (bf16[12,112,256]{2,1,0:T(8,128)(2,1)S(1)}, bf16[12,112,256]{2,1,0:T(8,128)(2,1)}, u32[]{:S(2)}, u32[]{:S(2)}) collective-permute-start(bf16[12,112,256]{2,1,0:T(8,128)(2,1)S(1)} %copy-done.6), channel_id=1, source_target_pairs={{0,208},{8,120},{16,224},{24,72},{32,240},{40,88},{48,192},{56,104... | collective-permute-start | bytes 2064392 | tf_op jit(solution)/shard_map/ppermute | solution.py:168
  117.1 41.1 %collective-permute-start.2 = (bf16[12,112,256]{2,1,0:T(8,128)(2,1)S(1)}, bf16[12,112,256]{2,1,0:T(8,128)(2,1)}, u32[]{:S(2)}, u32[]{:S(2)}) collective-permute-start(bf16[12,112,256]{2,1,0:T(8,128)(2,1)S(1)} %copy-done.5), channel_id=1, source_target_pairs={{0,128},{8,40},{16,144},{24,56},{32,160},{40,8},{48,176},{56,24},{... | collective-permute-start | bytes 2064392 | tf_op jit(solution)/shard_map/ppermute | solution.py:168
  131.1 12.8 %copy-start.14 = (bf16[12,112,256]{2,1,0:T(8,128)(2,1)}, bf16[12,112,256]{2,1,0:T(8,128)(2,1)S(1)}, u32[]{:S(2)}) copy-start(bf16[12,112,256]{2,1,0:T(8,128)(2,1)S(1)} %collective-permute-done.5.refs_3_) | copy-start | bytes 2064388
  167.5 23.8 %all-to-all-start = ((bf16[8,24,16,128]{3,2,1,0:T(8,128)(2,1)}), bf16[8,24,16,128]{3,2,1,0:T(8,128)(2,1)S(1)}, u32[]{:S(2)}, u32[]{:S(2)}) async-start(bf16[8,24,16,128]{3,2,1,0:T(8,128)(2,1)} %shard_map.75), calls=%async_computation | async-start | bytes 1572864 | tf_op jit(solution)/shard_map/all_to_all | solution.py:177
  175.3 16.1 %collective-permute-start.17 = (f32[24,16,128]{2,1,0:T(8,128)S(1)}, f32[24,16,128]{2,1,0:T(8,128)S(1)}, u32[]{:S(2)}, u32[]{:S(2)}) collective-permute-start(f32[24,16,128]{2,1,0:T(8,128)S(1)} %convert_reduce_fusion), channel_id=1, source_target_pairs={{0,160},{8,168},{16,176},{24,184},{32,128},{40,136},{48,144},{56,1... | collective-permute-start | bytes 589832 | tf_op jit(solution)/shard_map/ppermute | solution.py:180
  (7 other events, 35.8 us)

commit v2 on v1

--- a/solution.py
+++ b/solution.py
@@ -83,16 +83,16 @@
     return k + (with_right[:n] + with_right[n:]) + (with_left[:, :n] + with_left[:, n:])
 
 
-def kernel(count, first, last, pieces, slots_ref, w_ref, *refs):
+def kernel(count, first, last, pieces, facts_ref, d_ref, c_ref, *refs):
     blocks = refs[:count]
     out_ref = refs[-1]
-    v = w_ref.shape[1] - w_ref.shape[2]
-
     slots = blocks[0].shape[0] // 2
+    v, r = d_ref.shape[1:]
+    v = v - r if c_ref is None else v
 
     def partial_of(p):
-        i, j = slots_ref[p, 0], slots_ref[p, 1]
-        coeffs = jnp.concatenate([w_ref[2 * p, :v, :], w_ref[2 * p + 1, :v, :]], axis=1)
+        i, j = facts_ref[p, 0], facts_ref[p, 1]
+        coeffs = jnp.concatenate([d_ref[2 * p, :v, :], d_ref[2 * p + 1, :v, :]], axis=1)
         lefts = [b[half * slots + i] for b in blocks for half in range(2)]
         rights = [b[half * slots + j] for b in blocks for half in range(2)]
         total = contribution(lefts, rights, coeffs)
@@ -100,11 +100,18 @@
             total = [k + refs[count][2 * p + root] for root, k in enumerate(total)]
         return total
 
-    def store(at, k):
+    def store(p, root, k):
+        at = 2 * p + root
         if not last:
             out_ref[at] = k
             return
-        sigma = dress(k, w_ref[at, v:, :]).astype(jnp.bfloat16)
+        rank = facts_ref[p, 2 + root]
+        keep = (lax.broadcasted_iota(jnp.int32, k.shape, 0) < rank) & (
+            lax.broadcasted_iota(jnp.int32, k.shape, 1) < rank
+        )
+        amplitude = d_ref[at, v:, :] if c_ref is None else c_ref[at]
+        sigma = dress(jnp.where(keep, k, 0.0), amplitude)
+        sigma = jnp.where(keep, sigma, 0.0).astype(jnp.bfloat16)
         rows = sigma.shape[0] // pieces
         for piece in range(pieces):
             out_ref[piece, at] = sigma[piece * rows : (piece + 1) * rows]
@@ -113,50 +120,52 @@
         totals = [partial_of(step * TOGETHER + n) for n in range(TOGETHER)]
         for n, total in enumerate(totals):
             for root, k in enumerate(total):
-                store(2 * (step * TOGETHER + n) + root, k)
+                store(step * TOGETHER + n, root, k)
         return carry
 
-    lax.fori_loop(0, slots_ref.shape[0] // TOGETHER, pairs, 0)
-
-
-def accumulate(slots, w, blocks, total, last, pieces):
+    lax.fori_loop(0, facts_ref.shape[0] // TOGETHER, pairs, 0)
+
+
+def joint_kernel(count, first, last, pieces, facts_ref, w_ref, *refs):
+    kernel(count, first, last, pieces, facts_ref, w_ref, None, *refs)
+
+
+def accumulate(facts, coeffs, blocks, total, last, pieces):
     count, first = len(blocks), total is None
-    n, r = w.shape[0], w.shape[2]
+    n, r = coeffs[0].shape[0], coeffs[0].shape[2]
     shape = (pieces, n, r // pieces, r) if last else (n, r, r)
     dtype = jnp.bfloat16 if last else jnp.float32
-    operands = [w, *blocks] + ([] if first else [total])
+    operands = [*coeffs, *blocks] + ([] if first else [total])
     rows = 2 * count * blocks[0].shape[1]
-    v = w.shape[1] - r
+    v = blocks[0].shape[2]
     vmem = pl.BlockSpec(memory_space=pltpu.VMEM)
     return pl.pallas_call(
-        functools.partial(kernel, count, first, last, pieces),
+        functools.partial(kernel if len(coeffs) == 2 else joint_kernel, count, first, last, pieces),
         out_shape=jax.ShapeDtypeStruct(shape, dtype),
         in_specs=[pl.BlockSpec(memory_space=pltpu.SMEM)] + [vmem] * len(operands),
         out_specs=vmem,
         cost_estimate=pl.CostEstimate(
             flops=n * rows * r * (4 * v + 2 * r), bytes_accessed=2 * rows * 6 * v + 4 * n * r * r, transcendentals=0
         ),
-    )(slots, *operands)
+    )(facts, *operands)
 
 
 def per_device(panels, domain, pair_slots, ranks, transforms, trial):
     perms, targets = plan()
     partner = permutation(lambda x, y, core: (x + 2, y + 2, core))
-    partner_slots = lax.ppermute(pair_slots, "pairs", partner)
+    z, pieces = lax.axis_index("aux"), lax.axis_size("aux")
+    own_d = transforms.reshape((-1,) + transforms.shape[2:])
+    own_c = trial.reshape((-1,) + trial.shape[2:])
+    share = own_d.shape[0] // pieces
+    shard = [lax.dynamic_slice_in_dim(array, z * share, share, 0) for array in (own_d, own_c)]
+    shard = lax.ppermute(jnp.concatenate(shard, axis=1), "pairs", partner)
     sibling = lax.ppermute(panels, "pairs", permutation(lambda x, y, core: (x, y, 1 - core)))
-    z, pieces = lax.axis_index("aux"), lax.axis_size("aux")
-    width = transforms.shape[3]
-    keep = lax.broadcasted_iota(jnp.int32, ranks.shape + (width,), 2) < ranks[:, :, None]
-    masked_d = jnp.where(keep[:, :, None, :], transforms, jnp.zeros_like(transforms))
-    masked_c = jnp.where(keep[:, :, :, None] & keep[:, :, None, :], trial, jnp.zeros_like(trial))
-    own_w = jnp.concatenate([masked_d, masked_c], axis=2)
-    own_w = own_w.reshape(-1, own_w.shape[2], width)
-
-    share = own_w.shape[0] // pieces
-    shard = lax.ppermute(lax.dynamic_slice_in_dim(own_w, z * share, share, 0), "pairs", partner)
-    partner_w = lax.all_to_all(
+    facts = jnp.concatenate([pair_slots, ranks], axis=1)
+    partner_facts = lax.ppermute(facts, "pairs", partner)
+    spread = lax.all_to_all(
         jnp.broadcast_to(shard[None], (pieces,) + shard.shape), "aux", split_axis=0, concat_axis=0, tiled=True
-    ).reshape(own_w.shape)
+    )
+    partner_w = spread.reshape((-1,) + shard.shape[1:])
 
     mine = jnp.asarray(targets)[lax.axis_index("pairs")]
     rows_of = jnp.take(domain, mine, axis=0, mode="clip")
@@ -168,17 +177,17 @@
             row.append(lax.ppermute(blocks[step], "pairs", perms[step]))
         arrived.append(row)
 
-    def sums(side, slots, w):
+    def sums(side, facts, coeffs):
         total, at = None, 0
         for count in BATCHES[side]:
             last = at + count == len(perms)
-            total = accumulate(slots, w, arrived[side][at : at + count], total, last, pieces)
+            total = accumulate(facts, coeffs, arrived[side][at : at + count], total, last, pieces)
             at += count
         got = lax.all_to_all(total, "aux", split_axis=0, concat_axis=0, tiled=True)
         return got.astype(jnp.float32).sum(axis=0)
 
-    from_partner = lax.ppermute(sums(0, partner_slots, partner_w), "pairs", partner)
-    summed = (sums(1, pair_slots, own_w) + from_partner).astype(jnp.bfloat16)
+    from_partner = lax.ppermute(sums(0, partner_facts, (partner_w,)), "pairs", partner)
+    summed = (sums(1, facts, (own_d, own_c)) + from_partner).astype(jnp.bfloat16)
     return summed.reshape(ranks.shape + summed.shape[1:])
 
 

time: 195 us -> 198 us (1.015)
  the two profiles are of different devices: /device:TPU:12 before, /device:TPU:8 now
where the time goes in v2:
time: 198 us; the launch traced here: 197 us
  waiting for transfers between devices  85.5 us (43%)
  starting transfers between devices  52.7 us (27%)
  Pallas kernels  49.1 us (25%)
  local copies, waits for them, and re-layouts  9.05 us (5%)
    ppermute x14, waiting for transfers between devices, per_device(): row.append(lax.ppermute(blocks[step], 'pairs', perms[step]))  49.1 us
    pallas_call x3, Pallas kernels, accumulate(): pl.pallas_call(functools.partial(kernel if len(coeffs) == 2 else joint_ke...  37.2 us
    ppermute x14, starting transfers between devices, per_device(): row.append(lax.ppermute(blocks[step], 'pairs', perms[step]))  21.2 us
    all_to_all x2, waiting for transfers between devices, sums(): got = lax.all_to_all(total, 'aux', split_axis=0, concat_axis=0, tiled=True)  15.7 us
    all_to_all x2, starting transfers between devices, sums(): got = lax.all_to_all(total, 'aux', split_axis=0, concat_axis=0, tiled=True)  14.1 us
    ppermute x1, waiting for transfers between devices, per_device(): partner_facts = lax.ppermute(facts, 'pairs', partner)  12.2 us
    pallas_call x2, Pallas kernels, collect(): pl.pallas_call(collect_kernel, out_shape=[block] * steps, in_specs=[pl.Bl...  12 us
    all_to_all x1, starting transfers between devices, per_device(): lax.all_to_all(jnp.broadcast_to(shard[None], (pieces,) + shard.shape), 'a...  8.6 us
  transfers between devices with their start and end apart: 21, of which 6 were waited for; matrix products, arithmetic and copies ran while one was open for 3% of the time, Pallas kernels for 25%

profile of v2, /device:TPU:8, one launch (start us, length us, event | category | flops | bytes accessed | tf_op | source)
XLA Modules:
  0.0 197.4 jit_solution(3103037356866316293)
XLA Ops:
  0.0 0.9 constant_dynamic-slice_fusion
  0.9 0.9 constant_dynamic-slice_fusion.1
  1.9 4.8 %collective-permute-start.9 = (bf16[3,384,128]{2,1,0:T(8,128)(2,1)S(1)}, bf16[3,384,128]{2,1,0:T(8,128)(2,1)S(1)}, u32[]{:S(2)}, u32[]{:S(2)}) collective-permute-start(bf16[3,384,128]{2,1,0:T(8,128)(2,1)S(1)} %pad_maximum_fusion), channel_id=1, source_target_pairs={{0,160},{8,168},{16,176},{24,184},{32,128},{40,136},{48,144},{56,1... | collective-permute-start | bytes 884744 | tf_op jit(solution)/shard_map/ppermute | solution.py:161
  6.7 8.6 %collective-permute-done.9 = bf16[3,384,128]{2,1,0:T(8,128)(2,1)S(1)} collective-permute-done((bf16[3,384,128]{2,1,0:T(8,128)(2,1)S(1)}, bf16[3,384,128]{2,1,0:T(8,128)(2,1)S(1)}, u32[]{:S(2)}, u32[]{:S(2)}) %collective-permute-start.9) | collective-permute-done | bytes 294944 | tf_op jit(solution)/shard_map/ppermute | solution.py:161
  15.3 2.0 broadcast_in_dim.11
  17.2 8.6 %all-to-all-start.1 = ((bf16[8,3,384,128]{3,2,1,0:T(8,128)(2,1)}), bf16[8,3,384,128]{3,2,1,0:T(8,128)(2,1)S(1)}, u32[]{:S(2)}, u32[]{:S(2)}) async-start(bf16[8,3,384,128]{3,2,1,0:T(8,128)(2,1)} %broadcast_in_dim.11), calls=%async_computation.1 | async-start | bytes 4718592 | tf_op jit(solution)/shard_map/all_to_all | solution.py:165
  25.9 0.7 constant_dynamic-slice_fusion.2
  27.9 6.0 %shard_map.76 = (bf16[12,112,256]{2,1,0:T(8,128)(2,1)}, bf16[12,112,256]{2,1,0:T(8,128)(2,1)}, bf16[12,112,256]{2,1,0:T(8,128)(2,1)}, bf16[12,112,256]{2,1,0:T(8...) custom-call(s32[8,6]{1,0:T(8,128)} %get-tuple-element.37.rows_ref, ...), custom_call_target="tpu_custom_call" | custom-call | tf_op jit(solution)/shard_map/pallas_call | solution.py:56
  33.9 1.5 collective-permute-start.10
  35.4 1.7 collective-permute-start.11
  37.3 3.6 %collective-permute-start.8 = (s32[12,4]{1,0:T(8,128)S(1)}, s32[12,4]{1,0:T(8,128)S(1)}, u32[]{:S(2)}, u32[]{:S(2)}) collective-permute-start(s32[12,4]{1,0:T(8,128)S(1)} %copy.13.facts_ref), channel_id=1, source_target_pairs={{0,160},{8,168},{16,176},{24,184},{32,128},{40,136},{48,144},{56,1... | collective-permute-start | bytes 584 | tf_op jit(solution)/shard_map/ppermute | solution.py:164
  40.8 2.0 %collective-permute-start.13 = (bf16[12,112,256]{2,1,0:T(8,128)(2,1)}, bf16[12,112,256]{2,1,0:T(8,128)(2,1)}, u32[]{:S(2)}, u32[]{:S(2)}) collective-permute-start(bf16[12,112,256]{2,1,0:T(8,128)(2,1)} %get-tuple-element.33), channel_id=1, source_target_pairs={{0,48},{8,56},{16,0},{24,8},{32,16},{40,24},{48,32},{56,40},{64,11... | collective-permute-start | bytes 2064392 | tf_op jit(solution)/shard_map/ppermute | solution.py:177
  42.8 12.2 %collective-permute-done.8.facts_ref = s32[12,4]{1,0:T(8,128)S(1)} collective-permute-done((s32[12,4]{1,0:T(8,128)S(1)}, s32[12,4]{1,0:T(8,128)S(1)}, u32[]{:S(2)}, u32[]{:S(2)}) %collective-permute-start.8) | collective-permute-done | bytes 224 | tf_op jit(solution)/shard_map/ppermute | solution.py:164
  55.0 2.5 %collective-permute-start.14 = (bf16[12,112,256]{2,1,0:T(8,128)(2,1)}, bf16[12,112,256]{2,1,0:T(8,128)(2,1)}, u32[]{:S(2)}, u32[]{:S(2)}) collective-permute-start(bf16[12,112,256]{2,1,0:T(8,128)(2,1)} %get-tuple-element.34), channel_id=1, source_target_pairs={{0,240},{8,88},{16,192},{24,104},{32,208},{40,120},{48,224},{56,72... | collective-permute-start | bytes 2064392 | tf_op jit(solution)/shard_map/ppermute | solution.py:177
  57.5 2.5 %collective-permute-start.16 = (bf16[12,112,256]{2,1,0:T(8,128)(2,1)}, bf16[12,112,256]{2,1,0:T(8,128)(2,1)}, u32[]{:S(2)}, u32[]{:S(2)}) collective-permute-start(bf16[12,112,256]{2,1,0:T(8,128)(2,1)} %get-tuple-element.36), channel_id=1, source_target_pairs={{0,128},{8,40},{16,144},{24,56},{32,160},{40,8},{48,176},{56,24},{... | collective-permute-start | bytes 2064392 | tf_op jit(solution)/shard_map/ppermute | solution.py:177
  60.0 5.9 %shard_map.73 = (bf16[12,112,256]{2,1,0:T(8,128)(2,1)}, bf16[12,112,256]{2,1,0:T(8,128)(2,1)}, bf16[12,112,256]{2,1,0:T(8,128)(2,1)}, bf16[12,112,256]{2,1,0:T(8...) custom-call(s32[8,6]{1,0:T(8,128)} %get-tuple-element.38.rows_ref, ...), custom_call_target="tpu_custom_call" | custom-call | tf_op jit(solution)/shard_map/pallas_call | solution.py:56
  66.6 2.7 %collective-permute-start.4 = (bf16[12,112,256]{2,1,0:T(8,128)(2,1)}, bf16[12,112,256]{2,1,0:T(8,128)(2,1)}, u32[]{:S(2)}, u32[]{:S(2)}) collective-permute-start(bf16[12,112,256]{2,1,0:T(8,128)(2,1)} %get-tuple-element.25), channel_id=1, source_target_pairs={{0,192},{8,200},{16,208},{24,216},{32,224},{40,232},{48,240},{56,2... | collective-permute-start | bytes 2064392 | tf_op jit(solution)/shard_map/ppermute | solution.py:177
  69.3 20.1 %collective-permute-done.15.refs_6_ = bf16[12,112,256]{2,1,0:T(8,128)(2,1)} collective-permute-done((bf16[12,112,256]{2,1,0:T(8,128)(2,1)}, bf16[12,112,256]{2,1,0:T(8,128)(2,1)}, u32[]{:S(2)}, u32[]{:S(2)}) %collective-permute-start.15) | collective-permute-done | bytes 688160 | tf_op jit(solution)/shard_map/ppermute | solution.py:177
  89.4 1.4 copy-done
  90.9 15.2 %shard_map.77 = bf16[8,24,16,128]{3,2,1,0:T(8,128)(2,1)} custom-call(s32[12,4]{1,0:T(8,128)} %copy-done.12, bf16[24,384,128]{2,1,0:T(8,128)(2,1)} %bitcast.4, bf16[12,112,256]{2,1,0:T(8,128)(2,1)} %get-tuple-element.29.refs_0_, bf16[12,112,256]{2,1,0:T(8,128)(2,1)} %copy-done.8, bf16[12,112,256]{2,1,0:T(8,128)(2,1)} %collective-permute-done.11.refs_2_, ...), custom_call_target="tpu_custom_call" | custom-call | flops 7046430720 | bytes 7077888 | tf_op jit(solution)/shard_map/pallas_call | solution.py:142
  106.1 7.2 %all-to-all-start.2 = ((bf16[8,24,16,128]{3,2,1,0:T(8,128)(2,1)}), bf16[8,24,16,128]{3,2,1,0:T(8,128)(2,1)S(1)}, u32[]{:S(2)}, u32[]{:S(2)}) async-start(bf16[8,24,16,128]{3,2,1,0:T(8,128)(2,1)} %shard_map.77), calls=%async_computation.2 | async-start | bytes 1572864 | tf_op jit(solution)/shard_map/all_to_all | solution.py:186
  113.3 2.0 %collective-permute-start.6 = (bf16[12,112,256]{2,1,0:T(8,128)(2,1)}, bf16[12,112,256]{2,1,0:T(8,128)(2,1)S(1)}, u32[]{:S(2)}, u32[]{:S(2)}) collective-permute-start(bf16[12,112,256]{2,1,0:T(8,128)(2,1)} %get-tuple-element.27), channel_id=1, source_target_pairs={{0,48},{8,56},{16,0},{24,8},{32,16},{40,24},{48,32},{56,40},{64,11... | collective-permute-start | bytes 2064392 | tf_op jit(solution)/shard_map/ppermute | solution.py:177
  115.3 4.6 %collective-permute-start.7 = (bf16[12,112,256]{2,1,0:T(8,128)(2,1)S(1)}, bf16[12,112,256]{2,1,0:T(8,128)(2,1)S(1)}, u32[]{:S(2)}, u32[]{:S(2)}) collective-permute-start(bf16[12,112,256]{2,1,0:T(8,128)(2,1)S(1)} %copy-done.7), channel_id=1, source_target_pairs={{0,240},{8,88},{16,192},{24,104},{32,208},{40,120},{48,224},{56,72... | collective-permute-start | bytes 2064392 | tf_op jit(solution)/shard_map/ppermute | solution.py:177
  120.0 0.9 collective-permute-start.2
  120.9 23.6 %collective-permute-done.5.refs_3_ = bf16[12,112,256]{2,1,0:T(8,128)(2,1)S(1)} collective-permute-done((bf16[12,112,256]{2,1,0:T(8,128)(2,1)}, bf16[12,112,256]{2,1,0:T(8,128)(2,1)S(1)}, u32[]{:S(2)}, u32[]{:S(2)}) %collective-permute-start.5) | collective-permute-done | bytes 688160 | tf_op jit(solution)/shard_map/ppermute | solution.py:177
  144.5 5.4 %collective-permute-done.6.refs_4_ = bf16[12,112,256]{2,1,0:T(8,128)(2,1)S(1)} collective-permute-done((bf16[12,112,256]{2,1,0:T(8,128)(2,1)}, bf16[12,112,256]{2,1,0:T(8,128)(2,1)S(1)}, u32[]{:S(2)}, u32[]{:S(2)}) %collective-permute-start.6) | collective-permute-done | bytes 688160 | tf_op jit(solution)/shard_map/ppermute | solution.py:177
  149.9 0.8 copy-done.10
  150.7 0.9 copy-done.11
  151.6 12.6 %shard_map.74.refs_2_ = f32[24,128,128]{2,1,0:T(8,128)} custom-call(s32[12,4]{1,0:T(8,128)} %copy-done.1, bf16[24,256,128]{2,1,0:T(8,128)(2,1)} %bitcast.6, bf16[24,128,128]{2,1,0:T(8,128)(2,1)} %bitcast.9, bf16[12,112,256]{2,1,0:T(8,128)(2,1)} %get-tuple-element.23.refs_0_, bf16[12,112,256]{2,1,0:T(8,128)(2,1)} %collective-permute-done.3.refs_1_, ...), custom_call_target="tpu_custom_call" | custom-call | flops 5284823040 | bytes 5701632 | tf_op jit(solution)/shard_map/pallas_call | solution.py:142
  164.2 9.3 %shard_map.75 = bf16[8,24,16,128]{3,2,1,0:T(8,128)(2,1)} custom-call(s32[12,4]{1,0:T(8,128)} %copy-done.1, bf16[24,256,128]{2,1,0:T(8,128)(2,1)} %bitcast.7, bf16[24,128,128]{2,1,0:T(8,128)(2,1)} %bitcast.10, bf16[12,112,256]{2,1,0:T(8,128)(2,1)} %collective-permute-done.1.refs_0_, bf16[12,112,256]{2,1,0:T(8,128)(2,1)} %collective-permute-done.2.refs_1_, ...), custom_call_target="tpu_custom_call" | custom-call | flops 1761607680 | bytes 2949120 | tf_op jit(solution)/shard_map/pallas_call | solution.py:142
  173.5 7.0 %all-to-all-start = ((bf16[8,24,16,128]{3,2,1,0:T(8,128)(2,1)}), bf16[8,24,16,128]{3,2,1,0:T(8,128)(2,1)S(1)}, u32[]{:S(2)}, u32[]{:S(2)}) async-start(bf16[8,24,16,128]{3,2,1,0:T(8,128)(2,1)} %shard_map.75), calls=%async_computation | async-start | bytes 1572864 | tf_op jit(solution)/shard_map/all_to_all | solution.py:186
  180.9 15.7 %all-to-all-done = bf16[8,24,16,128]{3,2,1,0:T(8,128)(2,1)S(1)} async-done(((bf16[8,24,16,128]{3,2,1,0:T(8,128)(2,1)}), bf16[8,24,16,128]{3,2,1,0:T(8,128)(2,1)S(1)}, u32[]{:S(2)}, u32[]{:S(2)}) %all-to-all-start) | async-done | bytes 786464 | tf_op jit(solution)/shard_map/all_to_all | solution.py:186
  (56 shorter events, 3.4 us)
Async XLA Ops:
  0.0 27.9 %collective-permute-start = (bf16[64,112,256]{2,1,0:T(8,128)(2,1)}, bf16[64,112,256]{2,1,0:T(8,128)(2,1)}, u32[]{:S(2)}, u32[]{:S(2)}) collective-permute-start(bf16[64,112,256]{2,1,0:T(8,128)(2,1)} %panels_ref.3), channel_id=1, source_target_pairs={{0,8},{8,0},{16,24},{24,16},{32,40},{40,32},{48,56},{56,48},{64,72... | collective-permute-start | bytes 11010056 | tf_op jit(solution)/shard_map/ppermute | solution.py:162
  1.9 13.4 %collective-permute-start.9 = (bf16[3,384,128]{2,1,0:T(8,128)(2,1)S(1)}, bf16[3,384,128]{2,1,0:T(8,128)(2,1)S(1)}, u32[]{:S(2)}, u32[]{:S(2)}) collective-permute-start(bf16[3,384,128]{2,1,0:T(8,128)(2,1)S(1)} %pad_maximum_fusion), channel_id=1, source_target_pairs={{0,160},{8,168},{16,176},{24,184},{32,128},{40,136},{48,144},{56,1... | collective-permute-start | bytes 884744 | tf_op jit(solution)/shard_map/ppermute | solution.py:161
  17.2 8.6 %copy-start.2 = (s32[32,6]{0,1:T(8,128)S(1)}, s32[32,6]{0,1:T(8,128)}, u32[]{:S(2)}) copy-start(s32[32,6]{0,1:T(8,128)} %param.8) | copy-start | bytes 2308
  17.2 72.2 %all-to-all-start.1 = ((bf16[8,3,384,128]{3,2,1,0:T(8,128)(2,1)}), bf16[8,3,384,128]{3,2,1,0:T(8,128)(2,1)S(1)}, u32[]{:S(2)}, u32[]{:S(2)}) async-start(bf16[8,3,384,128]{3,2,1,0:T(8,128)(2,1)} %broadcast_in_dim.11), calls=%async_computation.1 | async-start | bytes 4718592 | tf_op jit(solution)/shard_map/all_to_all | solution.py:165
  27.9 9.3 %copy-start.3 = (s32[12,2]{0,1:T(2,128)S(1)}, s32[12,2]{0,1:T(2,128)}, u32[]{:S(2)}) copy-start(s32[12,2]{0,1:T(2,128)} %param.10) | copy-start | bytes 292
  27.9 9.3 %copy-start.4 = (s32[12,2]{0,1:T(2,128)S(1)}, s32[12,2]{0,1:T(2,128)}, u32[]{:S(2)}) copy-start(s32[12,2]{0,1:T(2,128)} %param.9) | copy-start | bytes 292
  33.9 23.6 %collective-permute-start.10 = (bf16[12,112,256]{2,1,0:T(8,128)(2,1)}, bf16[12,112,256]{2,1,0:T(8,128)(2,1)S(1)}, u32[]{:S(2)}, u32[]{:S(2)}) collective-permute-start(bf16[12,112,256]{2,1,0:T(8,128)(2,1)} %get-tuple-element.30), channel_id=1, source_target_pairs={{0,64},{8,72},{16,80},{24,88},{32,96},{40,104},{48,112},{56,120},{... | collective-permute-start | bytes 2064392 | tf_op jit(solution)/shard_map/ppermute | solution.py:177
  35.4 22.1 %collective-permute-start.11 = (bf16[12,112,256]{2,1,0:T(8,128)(2,1)}, bf16[12,112,256]{2,1,0:T(8,128)(2,1)}, u32[]{:S(2)}, u32[]{:S(2)}) collective-permute-start(bf16[12,112,256]{2,1,0:T(8,128)(2,1)} %get-tuple-element.31), channel_id=1, source_target_pairs={{0,192},{8,200},{16,208},{24,216},{32,224},{40,232},{48,240},{56,2... | collective-permute-start | bytes 2064392 | tf_op jit(solution)/shard_map/ppermute | solution.py:177
  37.3 28.7 %copy-start.1 = (s32[12,4]{1,0:T(8,128)}, s32[12,4]{1,0:T(8,128)S(1)}, u32[]{:S(2)}) copy-start(s32[12,4]{1,0:T(8,128)S(1)} %copy.13.facts_ref) | copy-start | bytes 580
  37.3 17.8 %collective-permute-start.8 = (s32[12,4]{1,0:T(8,128)S(1)}, s32[12,4]{1,0:T(8,128)S(1)}, u32[]{:S(2)}, u32[]{:S(2)}) collective-permute-start(s32[12,4]{1,0:T(8,128)S(1)} %copy.13.facts_ref), channel_id=1, source_target_pairs={{0,160},{8,168},{16,176},{24,184},{32,128},{40,136},{48,144},{56,1... | collective-permute-start | bytes 584 | tf_op jit(solution)/shard_map/ppermute | solution.py:164
  40.8 25.2 %collective-permute-start.12 = (bf16[12,112,256]{2,1,0:T(8,128)(2,1)}, bf16[12,112,256]{2,1,0:T(8,128)(2,1)}, u32[]{:S(2)}, u32[]{:S(2)}) collective-permute-start(bf16[12,112,256]{2,1,0:T(8,128)(2,1)} %get-tuple-element.32), channel_id=1, source_target_pairs={{0,16},{8,24},{16,32},{24,40},{32,48},{40,56},{48,0},{56,8},{64,80... | collective-permute-start | bytes 2064392 | tf_op jit(solution)/shard_map/ppermute | solution.py:177
  40.8 25.8 %collective-permute-start.13 = (bf16[12,112,256]{2,1,0:T(8,128)(2,1)}, bf16[12,112,256]{2,1,0:T(8,128)(2,1)}, u32[]{:S(2)}, u32[]{:S(2)}) collective-permute-start(bf16[12,112,256]{2,1,0:T(8,128)(2,1)} %get-tuple-element.33), channel_id=1, source_target_pairs={{0,48},{8,56},{16,0},{24,8},{32,16},{40,24},{48,32},{56,40},{64,11... | collective-permute-start | bytes 2064392 | tf_op jit(solution)/shard_map/ppermute | solution.py:177
  55.0 10.9 %copy-start.12 = (s32[12,4]{1,0:T(8,128)}, s32[12,4]{1,0:T(8,128)S(1)}, u32[]{:S(2)}) copy-start(s32[12,4]{1,0:T(8,128)S(1)} %collective-permute-done.8.facts_ref) | copy-start | bytes 580
  55.0 14.3 %collective-permute-start.14 = (bf16[12,112,256]{2,1,0:T(8,128)(2,1)}, bf16[12,112,256]{2,1,0:T(8,128)(2,1)}, u32[]{:S(2)}, u32[]{:S(2)}) collective-permute-start(bf16[12,112,256]{2,1,0:T(8,128)(2,1)} %get-tuple-element.34), channel_id=1, source_target_pairs={{0,240},{8,88},{16,192},{24,104},{32,208},{40,120},{48,224},{56,72... | collective-permute-start | bytes 2064392 | tf_op jit(solution)/shard_map/ppermute | solution.py:177
  57.5 8.5 %copy-start.8 = (bf16[12,112,256]{2,1,0:T(8,128)(2,1)}, bf16[12,112,256]{2,1,0:T(8,128)(2,1)S(1)}, u32[]{:S(2)}) copy-start(bf16[12,112,256]{2,1,0:T(8,128)(2,1)S(1)} %collective-permute-done.10.refs_1_) | copy-start | bytes 2064388
  57.5 31.9 %collective-permute-start.15 = (bf16[12,112,256]{2,1,0:T(8,128)(2,1)}, bf16[12,112,256]{2,1,0:T(8,128)(2,1)}, u32[]{:S(2)}, u32[]{:S(2)}) collective-permute-start(bf16[12,112,256]{2,1,0:T(8,128)(2,1)} %get-tuple-element.35), channel_id=1, source_target_pairs={{0,208},{8,120},{16,224},{24,72},{32,240},{40,88},{48,192},{56,104... | collective-permute-start | bytes 2064392 | tf_op jit(solution)/shard_map/ppermute | solution.py:177
  57.5 31.9 %collective-permute-start.16 = (bf16[12,112,256]{2,1,0:T(8,128)(2,1)}, bf16[12,112,256]{2,1,0:T(8,128)(2,1)}, u32[]{:S(2)}, u32[]{:S(2)}) collective-permute-start(bf16[12,112,256]{2,1,0:T(8,128)(2,1)} %get-tuple-element.36), channel_id=1, source_target_pairs={{0,128},{8,40},{16,144},{24,56},{32,160},{40,8},{48,176},{56,24},{... | collective-permute-start | bytes 2064392 | tf_op jit(solution)/shard_map/ppermute | solution.py:177
  66.0 53.9 %collective-permute-start.3 = (bf16[12,112,256]{2,1,0:T(8,128)(2,1)}, bf16[12,112,256]{2,1,0:T(8,128)(2,1)}, u32[]{:S(2)}, u32[]{:S(2)}) collective-permute-start(bf16[12,112,256]{2,1,0:T(8,128)(2,1)} %get-tuple-element.24), channel_id=1, source_target_pairs={{0,64},{8,72},{16,80},{24,88},{32,96},{40,104},{48,112},{56,120},{... | collective-permute-start | bytes 2064392 | tf_op jit(solution)/shard_map/ppermute | solution.py:177
  66.6 53.4 %collective-permute-start.4 = (bf16[12,112,256]{2,1,0:T(8,128)(2,1)}, bf16[12,112,256]{2,1,0:T(8,128)(2,1)}, u32[]{:S(2)}, u32[]{:S(2)}) collective-permute-start(bf16[12,112,256]{2,1,0:T(8,128)(2,1)} %get-tuple-element.25), channel_id=1, source_target_pairs={{0,192},{8,200},{16,208},{24,216},{32,224},{40,232},{48,240},{56,2... | collective-permute-start | bytes 2064392 | tf_op jit(solution)/shard_map/ppermute | solution.py:177
  89.4 1.4 copy-start
  90.9 24.4 %copy-start.7 = (bf16[12,112,256]{2,1,0:T(8,128)(2,1)S(1)}, bf16[12,112,256]{2,1,0:T(8,128)(2,1)}, u32[]{:S(2)}) copy-start(bf16[12,112,256]{2,1,0:T(8,128)(2,1)} %get-tuple-element.28) | copy-start | bytes 2064388
  106.1 13.8 %copy-start.6 = (bf16[12,112,256]{2,1,0:T(8,128)(2,1)S(1)}, bf16[12,112,256]{2,1,0:T(8,128)(2,1)}, u32[]{:S(2)}) copy-start(bf16[12,112,256]{2,1,0:T(8,128)(2,1)} %get-tuple-element.21) | copy-start | bytes 2064388
  106.1 13.9 %copy-start.5 = (bf16[12,112,256]{2,1,0:T(8,128)(2,1)S(1)}, bf16[12,112,256]{2,1,0:T(8,128)(2,1)}, u32[]{:S(2)}) copy-start(bf16[12,112,256]{2,1,0:T(8,128)(2,1)} %get-tuple-element.22) | copy-start | bytes 2064388
  106.1 67.4 %all-to-all-start.2 = ((bf16[8,24,16,128]{3,2,1,0:T(8,128)(2,1)}), bf16[8,24,16,128]{3,2,1,0:T(8,128)(2,1)S(1)}, u32[]{:S(2)}, u32[]{:S(2)}) async-start(bf16[8,24,16,128]{3,2,1,0:T(8,128)(2,1)} %shard_map.77), calls=%async_computation.2 | async-start | bytes 1572864 | tf_op jit(solution)/shard_map/all_to_all | solution.py:186
  113.3 31.2 %collective-permute-start.5 = (bf16[12,112,256]{2,1,0:T(8,128)(2,1)}, bf16[12,112,256]{2,1,0:T(8,128)(2,1)S(1)}, u32[]{:S(2)}, u32[]{:S(2)}) collective-permute-start(bf16[12,112,256]{2,1,0:T(8,128)(2,1)} %get-tuple-element.26), channel_id=1, source_target_pairs={{0,16},{8,24},{16,32},{24,40},{32,48},{40,56},{48,0},{56,8},{64,80... | collective-permute-start | bytes 2064392 | tf_op jit(solution)/shard_map/ppermute | solution.py:177
  113.3 36.6 %collective-permute-start.6 = (bf16[12,112,256]{2,1,0:T(8,128)(2,1)}, bf16[12,112,256]{2,1,0:T(8,128)(2,1)S(1)}, u32[]{:S(2)}, u32[]{:S(2)}) collective-permute-start(bf16[12,112,256]{2,1,0:T(8,128)(2,1)} %get-tuple-element.27), channel_id=1, source_target_pairs={{0,48},{8,56},{16,0},{24,8},{32,16},{40,24},{48,32},{56,40},{64,11... | collective-permute-start | bytes 2064392 | tf_op jit(solution)/shard_map/ppermute | solution.py:177
  115.3 34.6 %collective-permute-start.7 = (bf16[12,112,256]{2,1,0:T(8,128)(2,1)S(1)}, bf16[12,112,256]{2,1,0:T(8,128)(2,1)S(1)}, u32[]{:S(2)}, u32[]{:S(2)}) collective-permute-start(bf16[12,112,256]{2,1,0:T(8,128)(2,1)S(1)} %copy-done.7), channel_id=1, source_target_pairs={{0,240},{8,88},{16,192},{24,104},{32,208},{40,120},{48,224},{56,72... | collective-permute-start | bytes 2064392 | tf_op jit(solution)/shard_map/ppermute | solution.py:177
  119.9 44.3 %collective-permute-start.1 = (bf16[12,112,256]{2,1,0:T(8,128)(2,1)S(1)}, bf16[12,112,256]{2,1,0:T(8,128)(2,1)}, u32[]{:S(2)}, u32[]{:S(2)}) collective-permute-start(bf16[12,112,256]{2,1,0:T(8,128)(2,1)S(1)} %copy-done.6), channel_id=1, source_target_pairs={{0,208},{8,120},{16,224},{24,72},{32,240},{40,88},{48,192},{56,104... | collective-permute-start | bytes 2064392 | tf_op jit(solution)/shard_map/ppermute | solution.py:177
  120.0 44.2 %collective-permute-start.2 = (bf16[12,112,256]{2,1,0:T(8,128)(2,1)S(1)}, bf16[12,112,256]{2,1,0:T(8,128)(2,1)}, u32[]{:S(2)}, u32[]{:S(2)}) collective-permute-start(bf16[12,112,256]{2,1,0:T(8,128)(2,1)S(1)} %copy-done.5), channel_id=1, source_target_pairs={{0,128},{8,40},{16,144},{24,56},{32,160},{40,8},{48,176},{56,24},{... | collective-permute-start | bytes 2064392 | tf_op jit(solution)/shard_map/ppermute | solution.py:177
  144.5 5.4 %copy-start.9 = (bf16[12,112,256]{2,1,0:T(8,128)(2,1)}, bf16[12,112,256]{2,1,0:T(8,128)(2,1)S(1)}, u32[]{:S(2)}) copy-start(bf16[12,112,256]{2,1,0:T(8,128)(2,1)S(1)} %collective-permute-done.5.refs_3_) | copy-start | bytes 2064388
  173.5 23.1 %all-to-all-start = ((bf16[8,24,16,128]{3,2,1,0:T(8,128)(2,1)}), bf16[8,24,16,128]{3,2,1,0:T(8,128)(2,1)S(1)}, u32[]{:S(2)}, u32[]{:S(2)}) async-start(bf16[8,24,16,128]{3,2,1,0:T(8,128)(2,1)} %shard_map.75), calls=%async_computation | async-start | bytes 1572864 | tf_op jit(solution)/shard_map/all_to_all | solution.py:186
  180.6 16.1 %collective-permute-start.17 = (f32[24,16,128]{2,1,0:T(8,128)S(1)}, f32[24,16,128]{2,1,0:T(8,128)S(1)}, u32[]{:S(2)}, u32[]{:S(2)}) collective-permute-start(f32[24,16,128]{2,1,0:T(8,128)S(1)} %convert_reduce_fusion), channel_id=1, source_target_pairs={{0,160},{8,168},{16,176},{24,184},{32,128},{40,136},{48,144},{56,1... | collective-permute-start | bytes 589832 | tf_op jit(solution)/shard_map/ppermute | solution.py:189
  (2 other events, 1.7 us)

commit v3 on v2

--- a/solution.py
+++ b/solution.py
@@ -11,7 +11,7 @@
 
 SIDE = 4
 TOGETHER = 3
-BATCHES = ((8,), (6, 2))
+BATCHES = ((5, 3), (5, 3))
 
 STEPS = (
     ((0, 0), (1, 0), (-1, 0), (0, 1), (0, -1), (-1, -1), (-1, 1), (2, 0)),
@@ -126,28 +126,34 @@
     lax.fori_loop(0, facts_ref.shape[0] // TOGETHER, pairs, 0)
 
 
-def joint_kernel(count, first, last, pieces, facts_ref, w_ref, *refs):
+def joint_kernel(count, first, last, pieces, facts_ref, origins_ref, *refs):
+    shards, refs, w_ref = refs[:pieces], refs[pieces:-1], refs[-1]
+    share = shards[0].shape[0]
+    for n, shard_ref in enumerate(shards):
+        w_ref[pl.ds(origins_ref[n] * share, share)] = shard_ref[...]
     kernel(count, first, last, pieces, facts_ref, w_ref, None, *refs)
 
 
-def accumulate(facts, coeffs, blocks, total, last, pieces):
+def accumulate(facts, coeffs, blocks, total, last, pieces, origins=None):
     count, first = len(blocks), total is None
-    n, r = coeffs[0].shape[0], coeffs[0].shape[2]
+    n, r = 2 * facts.shape[0], coeffs[0].shape[2]
     shape = (pieces, n, r // pieces, r) if last else (n, r, r)
     dtype = jnp.bfloat16 if last else jnp.float32
     operands = [*coeffs, *blocks] + ([] if first else [total])
+    scalars = [facts] if origins is None else [facts, origins]
     rows = 2 * count * blocks[0].shape[1]
     v = blocks[0].shape[2]
     vmem = pl.BlockSpec(memory_space=pltpu.VMEM)
     return pl.pallas_call(
-        functools.partial(kernel if len(coeffs) == 2 else joint_kernel, count, first, last, pieces),
+        functools.partial(kernel if origins is None else joint_kernel, count, first, last, pieces),
         out_shape=jax.ShapeDtypeStruct(shape, dtype),
-        in_specs=[pl.BlockSpec(memory_space=pltpu.SMEM)] + [vmem] * len(operands),
+        in_specs=[pl.BlockSpec(memory_space=pltpu.SMEM)] * len(scalars) + [vmem] * len(operands),
         out_specs=vmem,
+        scratch_shapes=[] if origins is None else [pltpu.VMEM((n, v + r, r), coeffs[0].dtype)],
         cost_estimate=pl.CostEstimate(
             flops=n * rows * r * (4 * v + 2 * r), bytes_accessed=2 * rows * 6 * v + 4 * n * r * r, transcendentals=0
         ),
-    )(facts, *operands)
+    )(*scalars, *operands)
 
 
 def per_device(panels, domain, pair_slots, ranks, transforms, trial):
@@ -157,15 +163,21 @@
     own_d = transforms.reshape((-1,) + transforms.shape[2:])
     own_c = trial.reshape((-1,) + trial.shape[2:])
     share = own_d.shape[0] // pieces
+    sibling = lax.ppermute(panels, "pairs", permutation(lambda x, y, core: (x, y, 1 - core)))
     shard = [lax.dynamic_slice_in_dim(array, z * share, share, 0) for array in (own_d, own_c)]
     shard = lax.ppermute(jnp.concatenate(shard, axis=1), "pairs", partner)
-    sibling = lax.ppermute(panels, "pairs", permutation(lambda x, y, core: (x, y, 1 - core)))
     facts = jnp.concatenate([pair_slots, ranks], axis=1)
     partner_facts = lax.ppermute(facts, "pairs", partner)
-    spread = lax.all_to_all(
-        jnp.broadcast_to(shard[None], (pieces,) + shard.shape), "aux", split_axis=0, concat_axis=0, tiled=True
-    )
-    partner_w = spread.reshape((-1,) + shard.shape[1:])
+    shards, hops, up, down = [shard], [0], shard, shard
+    for hop in range(1, pieces // 2 + 1):
+        up = lax.ppermute(up, "aux", [(at, (at + 1) % pieces) for at in range(pieces)])
+        shards.append(up)
+        hops.append(-hop)
+        if 2 * hop < pieces:
+            down = lax.ppermute(down, "aux", [(at, (at - 1) % pieces) for at in range(pieces)])
+            shards.append(down)
+            hops.append(hop)
+    origins = (z + jnp.asarray(hops, jnp.int32)) % pieces
 
     mine = jnp.asarray(targets)[lax.axis_index("pairs")]
     rows_of = jnp.take(domain, mine, axis=0, mode="clip")
@@ -177,16 +189,16 @@
             row.append(lax.ppermute(blocks[step], "pairs", perms[step]))
         arrived.append(row)
 
-    def sums(side, facts, coeffs):
+    def sums(side, facts, coeffs, origins=None):
         total, at = None, 0
         for count in BATCHES[side]:
             last = at + count == len(perms)
-            total = accumulate(facts, coeffs, arrived[side][at : at + count], total, last, pieces)
+            total = accumulate(facts, coeffs, arrived[side][at : at + count], total, last, pieces, origins)
             at += count
         got = lax.all_to_all(total, "aux", split_axis=0, concat_axis=0, tiled=True)
         return got.astype(jnp.float32).sum(axis=0)
 
-    from_partner = lax.ppermute(sums(0, partner_facts, (partner_w,)), "pairs", partner)
+    from_partner = lax.ppermute(sums(0, partner_facts, shards, origins), "pairs", partner)
     summed = (sums(1, facts, (own_d, own_c)) + from_partner).astype(jnp.bfloat16)
     return summed.reshape(ranks.shape + summed.shape[1:])
 

time: 198 us -> 206 us (1.040)
  the two profiles are of different devices: /device:TPU:8 before, /device:TPU:12 now
where the time goes in v3:
time: 206 us; the launch traced here: 203 us
  waiting for transfers between devices  68.9 us (33%)
  starting transfers between devices  68.8 us (33%)
  Pallas kernels  55.6 us (27%)
  local copies, waits for them, and re-layouts  7.47 us (4%)
    pallas_call x4, Pallas kernels, accumulate(): pl.pallas_call(functools.partial(kernel if origins is None else joint_ker...  43.8 us
    ppermute x14, starting transfers between devices, per_device(): row.append(lax.ppermute(blocks[step], 'pairs', perms[step]))  34.1 us
    ppermute x14, waiting for transfers between devices, per_device(): row.append(lax.ppermute(blocks[step], 'pairs', perms[step]))  18.9 us
    ppermute x4, waiting for transfers between devices, per_device(): lax.ppermute(up, 'aux', [(at, (at + 1) % pieces) for at in range(pieces)])  18.5 us
    all_to_all x2, starting transfers between devices, sums(): got = lax.all_to_all(total, 'aux', split_axis=0, concat_axis=0, tiled=True)  12 us
    pallas_call x2, Pallas kernels, collect(): pl.pallas_call(collect_kernel, out_shape=[block] * steps, in_specs=[pl.Bl...  11.8 us
    all_to_all x2, waiting for transfers between devices, sums(): got = lax.all_to_all(total, 'aux', split_axis=0, concat_axis=0, tiled=True)  11.5 us
    ppermute x1, waiting for transfers between devices, per_device(): shard = lax.ppermute(jnp.concatenate(shard, axis=1), 'pairs', partner)  11.1 us
  transfers between devices with their start and end apart: 27, of which 9 were waited for; matrix products, arithmetic and copies ran while one was open for 3% of the time, Pallas kernels for 27%

profile of v3, /device:TPU:12, one launch (start us, length us, event | category | flops | bytes accessed | tf_op | source)
XLA Modules:
  0.0 202.5 jit_solution(5158917994231775735)
XLA Ops:
  1.9 2.3 %collective-permute-start.9 = (bf16[3,384,128]{2,1,0:T(8,128)(2,1)S(1)}, bf16[3,384,128]{2,1,0:T(8,128)(2,1)S(1)}, u32[]{:S(2)}, u32[]{:S(2)}) collective-permute-start(bf16[3,384,128]{2,1,0:T(8,128)(2,1)S(1)} %pad_maximum_fusion), channel_id=1, source_target_pairs={{0,160},{8,168},{16,176},{24,184},{32,128},{40,136},{48,144},{56,1... | collective-permute-start | bytes 884744 | tf_op jit(solution)/shard_map/ppermute | solution.py:168
  4.2 11.1 %collective-permute-done.9.refs_0_ = bf16[3,384,128]{2,1,0:T(8,128)(2,1)S(1)} collective-permute-done((bf16[3,384,128]{2,1,0:T(8,128)(2,1)S(1)}, bf16[3,384,128]{2,1,0:T(8,128)(2,1)S(1)}, u32[]{:S(2)}, u32[]{:S(2)}) %collective-permute-start.9) | collective-permute-done | bytes 294944 | tf_op jit(solution)/shard_map/ppermute | solution.py:168
  15.3 1.9 collective-permute-start.10
  17.2 3.9 %collective-permute-start.11 = (bf16[3,384,128]{2,1,0:T(8,128)(2,1)S(1)}, bf16[3,384,128]{2,1,0:T(8,128)(2,1)S(1)}, u32[]{:S(2)}, u32[]{:S(2)}) collective-permute-start(bf16[3,384,128]{2,1,0:T(8,128)(2,1)S(1)} %collective-permute-done.9.refs_0_), channel_id=1, source_target_pairs={{0,7},{1,0},{2,1},{3,2},{4,3},{5,4},{6,5},{7,6},{8,15},{9,8},{10,9... | collective-permute-start | bytes 884744 | tf_op jit(solution)/shard_map/ppermute | solution.py:177
  21.2 6.8 %collective-permute-done.10.refs_1_ = bf16[3,384,128]{2,1,0:T(8,128)(2,1)S(1)} collective-permute-done((bf16[3,384,128]{2,1,0:T(8,128)(2,1)S(1)}, bf16[3,384,128]{2,1,0:T(8,128)(2,1)S(1)}, u32[]{:S(2)}, u32[]{:S(2)}) %collective-permute-start.10) | collective-permute-done | bytes 294944 | tf_op jit(solution)/shard_map/ppermute | solution.py:173
  30.1 3.3 %collective-permute-start.13 = (bf16[3,384,128]{2,1,0:T(8,128)(2,1)S(1)}, bf16[3,384,128]{2,1,0:T(8,128)(2,1)S(1)}, u32[]{:S(2)}, u32[]{:S(2)}) collective-permute-start(bf16[3,384,128]{2,1,0:T(8,128)(2,1)S(1)} %collective-permute-done.11.refs_2_), channel_id=1, source_target_pairs={{0,7},{1,0},{2,1},{3,2},{4,3},{5,4},{6,5},{7,6},{8,15},{9,8},{10,9... | collective-permute-start | bytes 884744 | tf_op jit(solution)/shard_map/ppermute | solution.py:177
  33.4 3.8 %collective-permute-done.12.refs_3_ = bf16[3,384,128]{2,1,0:T(8,128)(2,1)S(1)} collective-permute-done((bf16[3,384,128]{2,1,0:T(8,128)(2,1)S(1)}, bf16[3,384,128]{2,1,0:T(8,128)(2,1)S(1)}, u32[]{:S(2)}, u32[]{:S(2)}) %collective-permute-start.12) | collective-permute-done | bytes 294944 | tf_op jit(solution)/shard_map/ppermute | solution.py:173
  37.8 5.9 %shard_map.85 = (bf16[12,112,256]{2,1,0:T(8,128)(2,1)}, bf16[12,112,256]{2,1,0:T(8,128)(2,1)}, bf16[12,112,256]{2,1,0:T(8,128)(2,1)}, bf16[12,112,256]{2,1,0:T(8...) custom-call(s32[8,6]{1,0:T(8,128)} %get-tuple-element.37.rows_ref, ...), custom_call_target="tpu_custom_call" | custom-call | tf_op jit(solution)/shard_map/pallas_call | solution.py:56
  45.9 3.2 %collective-permute-start.15 = (bf16[3,384,128]{2,1,0:T(8,128)(2,1)S(1)}, bf16[3,384,128]{2,1,0:T(8,128)(2,1)}, u32[]{:S(2)}, u32[]{:S(2)}) collective-permute-start(bf16[3,384,128]{2,1,0:T(8,128)(2,1)S(1)} %collective-permute-done.13.refs_4_), channel_id=1, source_target_pairs={{0,7},{1,0},{2,1},{3,2},{4,3},{5,4},{6,5},{7,6},{8,15},{9,8},{10,9... | collective-permute-start | bytes 884744 | tf_op jit(solution)/shard_map/ppermute | solution.py:177
  49.2 3.5 %collective-permute-start.8 = (s32[12,4]{1,0:T(8,128)S(1)}, s32[12,4]{1,0:T(8,128)S(1)}, u32[]{:S(2)}, u32[]{:S(2)}) collective-permute-start(s32[12,4]{1,0:T(8,128)S(1)} %copy.14.facts_ref), channel_id=1, source_target_pairs={{0,160},{8,168},{16,176},{24,184},{32,128},{40,136},{48,144},{56,1... | collective-permute-start | bytes 584 | tf_op jit(solution)/shard_map/ppermute | solution.py:170
  52.6 8.9 %collective-permute-done.8.facts_ref = s32[12,4]{1,0:T(8,128)S(1)} collective-permute-done((s32[12,4]{1,0:T(8,128)S(1)}, s32[12,4]{1,0:T(8,128)S(1)}, u32[]{:S(2)}, u32[]{:S(2)}) %collective-permute-start.8) | collective-permute-done | bytes 224 | tf_op jit(solution)/shard_map/ppermute | solution.py:170
  61.5 2.0 collective-permute-start.23
  63.5 7.9 %collective-permute-done.16.refs_7_ = bf16[3,384,128]{2,1,0:T(8,128)(2,1)S(1)} collective-permute-done((bf16[3,384,128]{2,1,0:T(8,128)(2,1)S(1)}, bf16[3,384,128]{2,1,0:T(8,128)(2,1)S(1)}, u32[]{:S(2)}, u32[]{:S(2)}) %collective-permute-start.16) | collective-permute-done | bytes 294944 | tf_op jit(solution)/shard_map/ppermute | solution.py:173
  72.2 4.4 %collective-permute-start.17 = (bf16[12,112,256]{2,1,0:T(8,128)(2,1)}, bf16[12,112,256]{2,1,0:T(8,128)(2,1)S(1)}, u32[]{:S(2)}, u32[]{:S(2)}) collective-permute-start(bf16[12,112,256]{2,1,0:T(8,128)(2,1)} %get-tuple-element.29), channel_id=1, source_target_pairs={{0,240},{8,88},{16,192},{24,104},{32,208},{40,120},{48,224},{56,72... | collective-permute-start | bytes 2064392 | tf_op jit(solution)/shard_map/ppermute | solution.py:189
  76.9 2.2 %collective-permute-start.19 = (bf16[12,112,256]{2,1,0:T(8,128)(2,1)}, bf16[12,112,256]{2,1,0:T(8,128)(2,1)}, u32[]{:S(2)}, u32[]{:S(2)}) collective-permute-start(bf16[12,112,256]{2,1,0:T(8,128)(2,1)} %get-tuple-element.31), channel_id=1, source_target_pairs={{0,128},{8,40},{16,144},{24,56},{32,160},{40,8},{48,176},{56,24},{... | collective-permute-start | bytes 2064392 | tf_op jit(solution)/shard_map/ppermute | solution.py:189
  79.7 5.9 %shard_map.82 = (bf16[12,112,256]{2,1,0:T(8,128)(2,1)}, bf16[12,112,256]{2,1,0:T(8,128)(2,1)}, bf16[12,112,256]{2,1,0:T(8,128)(2,1)}, bf16[12,112,256]{2,1,0:T(8...) custom-call(s32[8,6]{1,0:T(8,128)} %get-tuple-element.38.rows_ref, ...), custom_call_target="tpu_custom_call" | custom-call | tf_op jit(solution)/shard_map/pallas_call | solution.py:56
  86.5 3.4 %collective-permute-start.4 = (bf16[12,112,256]{2,1,0:T(8,128)(2,1)}, bf16[12,112,256]{2,1,0:T(8,128)(2,1)}, u32[]{:S(2)}, u32[]{:S(2)}) collective-permute-start(bf16[12,112,256]{2,1,0:T(8,128)(2,1)} %get-tuple-element.25), channel_id=1, source_target_pairs={{0,64},{8,72},{16,80},{24,88},{32,96},{40,104},{48,112},{56,120},{... | collective-permute-start | bytes 2064392 | tf_op jit(solution)/shard_map/ppermute | solution.py:189
  89.8 6.3 %collective-permute-start.5 = (bf16[12,112,256]{2,1,0:T(8,128)(2,1)}, bf16[12,112,256]{2,1,0:T(8,128)(2,1)}, u32[]{:S(2)}, u32[]{:S(2)}) collective-permute-start(bf16[12,112,256]{2,1,0:T(8,128)(2,1)} %get-tuple-element.26), channel_id=1, source_target_pairs={{0,192},{8,200},{16,208},{24,216},{32,224},{40,232},{48,240},{56,2... | collective-permute-start | bytes 2064392 | tf_op jit(solution)/shard_map/ppermute | solution.py:189
  96.2 11.4 %shard_map.86.refs_11_ = f32[24,128,128]{2,1,0:T(8,128)} custom-call(s32[12,4]{1,0:T(8,128)} %copy-done.21, s32[8]{0:T(128)} %and_select_fusion.origins_ref, bf16[3,384,128]{2,1,0:T(8,128)(2,1)} %copy-done.14, bf16[3,384,128]{2,1,0:T(8,128)(2,1)} %copy-done.15, bf16[3,384,128]{2,1,0:T(8,128)(2,1)} %copy-done.16, bf16[3,384,128]{2,1,0:T(8,128)(2,1)} %copy-done.17, ...), custom_call_target="tpu_custom_call" | custom-call | flops 4404019200 | bytes 5013504 | tf_op jit(solution)/shard_map/pallas_call | solution.py:147
  108.8 10.7 %shard_map.87 = bf16[8,24,16,128]{3,2,1,0:T(8,128)(2,1)} custom-call(s32[12,4]{1,0:T(8,128)} %copy-done.21, s32[8]{0:T(128)} %and_select_fusion.origins_ref, bf16[3,384,128]{2,1,0:T(8,128)(2,1)} %copy-done.14, bf16[3,384,128]{2,1,0:T(8,128)(2,1)} %copy-done.15, bf16[3,384,128]{2,1,0:T(8,128)(2,1)} %copy-done.16, bf16[3,384,128]{2,1,0:T(8,128)(2,1)} %copy-done.17, ...), custom_call_target="tpu_custom_call" | custom-call | flops 2642411520 | bytes 3637248 | tf_op jit(solution)/shard_map/pallas_call | solution.py:147
  119.5 5.1 %all-to-all-start.1 = ((bf16[8,24,16,128]{3,2,1,0:T(8,128)(2,1)}), bf16[8,24,16,128]{3,2,1,0:T(8,128)(2,1)S(1)}, u32[]{:S(2)}, u32[]{:S(2)}) async-start(bf16[8,24,16,128]{3,2,1,0:T(8,128)(2,1)} %shard_map.87), calls=%async_computation.1 | async-start | bytes 1572864 | tf_op jit(solution)/shard_map/all_to_all | solution.py:198
  124.5 3.0 %collective-permute-start.6 = (bf16[12,112,256]{2,1,0:T(8,128)(2,1)}, bf16[12,112,256]{2,1,0:T(8,128)(2,1)S(1)}, u32[]{:S(2)}, u32[]{:S(2)}) collective-permute-start(bf16[12,112,256]{2,1,0:T(8,128)(2,1)} %get-tuple-element.27), channel_id=1, source_target_pairs={{0,16},{8,24},{16,32},{24,40},{32,48},{40,56},{48,0},{56,8},{64,80... | collective-permute-start | bytes 2064392 | tf_op jit(solution)/shard_map/ppermute | solution.py:189
  127.5 3.7 %collective-permute-start.7 = (bf16[12,112,256]{2,1,0:T(8,128)(2,1)S(1)}, bf16[12,112,256]{2,1,0:T(8,128)(2,1)S(1)}, u32[]{:S(2)}, u32[]{:S(2)}) collective-permute-start(bf16[12,112,256]{2,1,0:T(8,128)(2,1)S(1)} %copy-done.7), channel_id=1, source_target_pairs={{0,48},{8,56},{16,0},{24,8},{32,16},{40,24},{48,32},{56,40},{64,11... | collective-permute-start | bytes 2064392 | tf_op jit(solution)/shard_map/ppermute | solution.py:189
  131.3 4.5 %collective-permute-start.1 = (bf16[12,112,256]{2,1,0:T(8,128)(2,1)S(1)}, bf16[12,112,256]{2,1,0:T(8,128)(2,1)}, u32[]{:S(2)}, u32[]{:S(2)}) collective-permute-start(bf16[12,112,256]{2,1,0:T(8,128)(2,1)S(1)} %copy-done.5), channel_id=1, source_target_pairs={{0,240},{8,88},{16,192},{24,104},{32,208},{40,120},{48,224},{56,72... | collective-permute-start | bytes 2064392 | tf_op jit(solution)/shard_map/ppermute | solution.py:189
  136.5 1.5 collective-permute-start.3
  138.0 16.7 %collective-permute-done.6.refs_3_ = bf16[12,112,256]{2,1,0:T(8,128)(2,1)S(1)} collective-permute-done((bf16[12,112,256]{2,1,0:T(8,128)(2,1)}, bf16[12,112,256]{2,1,0:T(8,128)(2,1)S(1)}, u32[]{:S(2)}, u32[]{:S(2)}) %collective-permute-start.6) | collective-permute-done | bytes 688160 | tf_op jit(solution)/shard_map/ppermute | solution.py:189
  154.7 1.4 collective-permute-done.7.refs_4_
  157.0 11.3 %shard_map.83.refs_3_ = f32[24,128,128]{2,1,0:T(8,128)} custom-call(s32[12,4]{1,0:T(8,128)} %copy-done, bf16[24,256,128]{2,1,0:T(8,128)(2,1)} %bitcast.4, bf16[24,128,128]{2,1,0:T(8,128)(2,1)} %bitcast.7, bf16[12,112,256]{2,1,0:T(8,128)(2,1)} %get-tuple-element.24.refs_0_, bf16[12,112,256]{2,1,0:T(8,128)(2,1)} %collective-permute-done.4.refs_1_, ...), custom_call_target="tpu_custom_call" | custom-call | flops 4404019200 | bytes 5013504 | tf_op jit(solution)/shard_map/pallas_call | solution.py:147
  168.3 10.4 %shard_map.84 = bf16[8,24,16,128]{3,2,1,0:T(8,128)(2,1)} custom-call(s32[12,4]{1,0:T(8,128)} %copy-done, bf16[24,256,128]{2,1,0:T(8,128)(2,1)} %bitcast.5, bf16[24,128,128]{2,1,0:T(8,128)(2,1)} %bitcast.8, bf16[12,112,256]{2,1,0:T(8,128)(2,1)} %collective-permute-done.1.refs_0_, bf16[12,112,256]{2,1,0:T(8,128)(2,1)} %collective-permute-done.2.refs_1_, ...), custom_call_target="tpu_custom_call" | custom-call | flops 2642411520 | bytes 3637248 | tf_op jit(solution)/shard_map/pallas_call | solution.py:147
  178.7 6.9 %all-to-all-start = ((bf16[8,24,16,128]{3,2,1,0:T(8,128)(2,1)}), bf16[8,24,16,128]{3,2,1,0:T(8,128)(2,1)S(1)}, u32[]{:S(2)}, u32[]{:S(2)}) async-start(bf16[8,24,16,128]{3,2,1,0:T(8,128)(2,1)} %shard_map.84), calls=%async_computation | async-start | bytes 1572864 | tf_op jit(solution)/shard_map/all_to_all | solution.py:198
  185.7 4.6 %collective-permute-start.24 = (f32[24,16,128]{2,1,0:T(8,128)S(1)}, f32[24,16,128]{2,1,0:T(8,128)S(1)}, u32[]{:S(2)}, u32[]{:S(2)}) collective-permute-start(f32[24,16,128]{2,1,0:T(8,128)S(1)} %convert_reduce_fusion), channel_id=1, source_target_pairs={{0,160},{8,168},{16,176},{24,184},{32,128},{40,136},{48,144},{56,1... | collective-permute-start | bytes 589832 | tf_op jit(solution)/shard_map/ppermute | solution.py:201
  190.3 11.5 %all-to-all-done = bf16[8,24,16,128]{3,2,1,0:T(8,128)(2,1)S(1)} async-done(((bf16[8,24,16,128]{3,2,1,0:T(8,128)(2,1)}), bf16[8,24,16,128]{3,2,1,0:T(8,128)(2,1)S(1)}, u32[]{:S(2)}, u32[]{:S(2)}) %all-to-all-start) | async-done | bytes 786464 | tf_op jit(solution)/shard_map/all_to_all | solution.py:198
  (89 shorter events, 13.0 us)
Async XLA Ops:
  0.0 37.8 %collective-permute-start = (bf16[64,112,256]{2,1,0:T(8,128)(2,1)}, bf16[64,112,256]{2,1,0:T(8,128)(2,1)}, u32[]{:S(2)}, u32[]{:S(2)}) collective-permute-start(bf16[64,112,256]{2,1,0:T(8,128)(2,1)} %panels_ref.3), channel_id=1, source_target_pairs={{0,8},{8,0},{16,24},{24,16},{32,40},{40,32},{48,56},{56,48},{64,72... | collective-permute-start | bytes 11010056 | tf_op jit(solution)/shard_map/ppermute | solution.py:166
  1.9 13.4 %collective-permute-start.9 = (bf16[3,384,128]{2,1,0:T(8,128)(2,1)S(1)}, bf16[3,384,128]{2,1,0:T(8,128)(2,1)S(1)}, u32[]{:S(2)}, u32[]{:S(2)}) collective-permute-start(bf16[3,384,128]{2,1,0:T(8,128)(2,1)S(1)} %pad_maximum_fusion), channel_id=1, source_target_pairs={{0,160},{8,168},{16,176},{24,184},{32,128},{40,136},{48,144},{56,1... | collective-permute-start | bytes 884744 | tf_op jit(solution)/shard_map/ppermute | solution.py:168
  15.3 28.4 %copy-start.14 = (bf16[3,384,128]{2,1,0:T(8,128)(2,1)}, bf16[3,384,128]{2,1,0:T(8,128)(2,1)S(1)}, u32[]{:S(2)}) copy-start(bf16[3,384,128]{2,1,0:T(8,128)(2,1)S(1)} %collective-permute-done.9.refs_0_) | copy-start | bytes 884740
  15.3 12.7 %collective-permute-start.10 = (bf16[3,384,128]{2,1,0:T(8,128)(2,1)S(1)}, bf16[3,384,128]{2,1,0:T(8,128)(2,1)S(1)}, u32[]{:S(2)}, u32[]{:S(2)}) collective-permute-start(bf16[3,384,128]{2,1,0:T(8,128)(2,1)S(1)} %collective-permute-done.9.refs_0_), channel_id=1, source_target_pairs={{0,1},{1,2},{2,3},{3,4},{4,5},{5,6},{6,7},{7,0},{8,9},{9,10},{10,1... | collective-permute-start | bytes 884744 | tf_op jit(solution)/shard_map/ppermute | solution.py:173
  17.2 12.9 %collective-permute-start.11 = (bf16[3,384,128]{2,1,0:T(8,128)(2,1)S(1)}, bf16[3,384,128]{2,1,0:T(8,128)(2,1)S(1)}, u32[]{:S(2)}, u32[]{:S(2)}) collective-permute-start(bf16[3,384,128]{2,1,0:T(8,128)(2,1)S(1)} %collective-permute-done.9.refs_0_), channel_id=1, source_target_pairs={{0,7},{1,0},{2,1},{3,2},{4,3},{5,4},{6,5},{7,6},{8,15},{9,8},{10,9... | collective-permute-start | bytes 884744 | tf_op jit(solution)/shard_map/ppermute | solution.py:177
  28.0 9.2 %collective-permute-start.12 = (bf16[3,384,128]{2,1,0:T(8,128)(2,1)S(1)}, bf16[3,384,128]{2,1,0:T(8,128)(2,1)S(1)}, u32[]{:S(2)}, u32[]{:S(2)}) collective-permute-start(bf16[3,384,128]{2,1,0:T(8,128)(2,1)S(1)} %collective-permute-done.10.refs_1_), channel_id=1, source_target_pairs={{0,1},{1,2},{2,3},{3,4},{4,5},{5,6},{6,7},{7,0},{8,9},{9,10},{10,1... | collective-permute-start | bytes 884744 | tf_op jit(solution)/shard_map/ppermute | solution.py:173
  30.1 15.8 %collective-permute-start.13 = (bf16[3,384,128]{2,1,0:T(8,128)(2,1)S(1)}, bf16[3,384,128]{2,1,0:T(8,128)(2,1)S(1)}, u32[]{:S(2)}, u32[]{:S(2)}) collective-permute-start(bf16[3,384,128]{2,1,0:T(8,128)(2,1)S(1)} %collective-permute-done.11.refs_2_), channel_id=1, source_target_pairs={{0,7},{1,0},{2,1},{3,2},{4,3},{5,4},{6,5},{7,6},{8,15},{9,8},{10,9... | collective-permute-start | bytes 884744 | tf_op jit(solution)/shard_map/ppermute | solution.py:177
  37.2 24.3 %collective-permute-start.14 = (bf16[3,384,128]{2,1,0:T(8,128)(2,1)S(1)}, bf16[3,384,128]{2,1,0:T(8,128)(2,1)S(1)}, u32[]{:S(2)}, u32[]{:S(2)}) collective-permute-start(bf16[3,384,128]{2,1,0:T(8,128)(2,1)S(1)} %collective-permute-done.12.refs_3_), channel_id=1, source_target_pairs={{0,1},{1,2},{2,3},{3,4},{4,5},{5,6},{6,7},{7,0},{8,9},{9,10},{10,1... | collective-permute-start | bytes 884744 | tf_op jit(solution)/shard_map/ppermute | solution.py:173
  37.8 41.3 %copy-start.22 = (s32[8]{0:T(128)S(1)}, s32[8]{0:T(128)}, u32[]{:S(2)}) copy-start(s32[8]{0:T(128)} %constant.37.clone) | copy-start | bytes 100
  43.8 32.8 %collective-permute-start.20 = (bf16[12,112,256]{2,1,0:T(8,128)(2,1)}, bf16[12,112,256]{2,1,0:T(8,128)(2,1)S(1)}, u32[]{:S(2)}, u32[]{:S(2)}) collective-permute-start(bf16[12,112,256]{2,1,0:T(8,128)(2,1)} %get-tuple-element.33), channel_id=1, source_target_pairs={{0,64},{8,72},{16,80},{24,88},{32,96},{40,104},{48,112},{56,120},{... | collective-permute-start | bytes 2064392 | tf_op jit(solution)/shard_map/ppermute | solution.py:189
  45.0 31.8 %collective-permute-start.21 = (bf16[12,112,256]{2,1,0:T(8,128)(2,1)}, bf16[12,112,256]{2,1,0:T(8,128)(2,1)S(1)}, u32[]{:S(2)}, u32[]{:S(2)}) collective-permute-start(bf16[12,112,256]{2,1,0:T(8,128)(2,1)} %get-tuple-element.34), channel_id=1, source_target_pairs={{0,192},{8,200},{16,208},{24,216},{32,224},{40,232},{48,240},{56,2... | collective-permute-start | bytes 2064392 | tf_op jit(solution)/shard_map/ppermute | solution.py:189
  45.9 30.7 %copy-start.18 = (bf16[3,384,128]{2,1,0:T(8,128)(2,1)}, bf16[3,384,128]{2,1,0:T(8,128)(2,1)S(1)}, u32[]{:S(2)}) copy-start(bf16[3,384,128]{2,1,0:T(8,128)(2,1)S(1)} %collective-permute-done.13.refs_4_) | copy-start | bytes 884740
  45.9 17.7 %collective-permute-start.15 = (bf16[3,384,128]{2,1,0:T(8,128)(2,1)S(1)}, bf16[3,384,128]{2,1,0:T(8,128)(2,1)}, u32[]{:S(2)}, u32[]{:S(2)}) collective-permute-start(bf16[3,384,128]{2,1,0:T(8,128)(2,1)S(1)} %collective-permute-done.13.refs_4_), channel_id=1, source_target_pairs={{0,7},{1,0},{2,1},{3,2},{4,3},{5,4},{6,5},{7,6},{8,15},{9,8},{10,9... | collective-permute-start | bytes 884744 | tf_op jit(solution)/shard_map/ppermute | solution.py:177
  49.2 36.5 %copy-start = (s32[12,4]{1,0:T(8,128)}, s32[12,4]{1,0:T(8,128)S(1)}, u32[]{:S(2)}) copy-start(s32[12,4]{1,0:T(8,128)S(1)} %copy.14.facts_ref) | copy-start | bytes 580
  49.2 12.3 %collective-permute-start.8 = (s32[12,4]{1,0:T(8,128)S(1)}, s32[12,4]{1,0:T(8,128)S(1)}, u32[]{:S(2)}, u32[]{:S(2)}) collective-permute-start(s32[12,4]{1,0:T(8,128)S(1)} %copy.14.facts_ref), channel_id=1, source_target_pairs={{0,160},{8,168},{16,176},{24,184},{32,128},{40,136},{48,144},{56,1... | collective-permute-start | bytes 584 | tf_op jit(solution)/shard_map/ppermute | solution.py:170
  61.5 34.6 %copy-start.21 = (s32[12,4]{1,0:T(8,128)}, s32[12,4]{1,0:T(8,128)S(1)}, u32[]{:S(2)}) copy-start(s32[12,4]{1,0:T(8,128)S(1)} %collective-permute-done.8.facts_ref) | copy-start | bytes 580
  61.5 24.9 %collective-permute-start.22 = (bf16[12,112,256]{2,1,0:T(8,128)(2,1)}, bf16[12,112,256]{2,1,0:T(8,128)(2,1)S(1)}, u32[]{:S(2)}, u32[]{:S(2)}) collective-permute-start(bf16[12,112,256]{2,1,0:T(8,128)(2,1)} %get-tuple-element.35), channel_id=1, source_target_pairs={{0,16},{8,24},{16,32},{24,40},{32,48},{40,56},{48,0},{56,8},{64,80... | collective-permute-start | bytes 2064392 | tf_op jit(solution)/shard_map/ppermute | solution.py:189
  61.5 28.3 %collective-permute-start.23 = (bf16[12,112,256]{2,1,0:T(8,128)(2,1)}, bf16[12,112,256]{2,1,0:T(8,128)(2,1)}, u32[]{:S(2)}, u32[]{:S(2)}) collective-permute-start(bf16[12,112,256]{2,1,0:T(8,128)(2,1)} %get-tuple-element.36), channel_id=1, source_target_pairs={{0,48},{8,56},{16,0},{24,8},{32,16},{40,24},{48,32},{56,40},{64,11... | collective-permute-start | bytes 2064392 | tf_op jit(solution)/shard_map/ppermute | solution.py:189
  63.5 7.9 %collective-permute-start.16 = (bf16[3,384,128]{2,1,0:T(8,128)(2,1)S(1)}, bf16[3,384,128]{2,1,0:T(8,128)(2,1)S(1)}, u32[]{:S(2)}, u32[]{:S(2)}) collective-permute-start(bf16[3,384,128]{2,1,0:T(8,128)(2,1)S(1)} %collective-permute-done.14.refs_5_), channel_id=1, source_target_pairs={{0,1},{1,2},{2,3},{3,4},{4,5},{5,6},{6,7},{7,0},{8,9},{9,10},{10,1... | collective-permute-start | bytes 884744 | tf_op jit(solution)/shard_map/ppermute | solution.py:173
  72.2 35.4 %collective-permute-start.17 = (bf16[12,112,256]{2,1,0:T(8,128)(2,1)}, bf16[12,112,256]{2,1,0:T(8,128)(2,1)S(1)}, u32[]{:S(2)}, u32[]{:S(2)}) collective-permute-start(bf16[12,112,256]{2,1,0:T(8,128)(2,1)} %get-tuple-element.29), channel_id=1, source_target_pairs={{0,240},{8,88},{16,192},{24,104},{32,208},{40,120},{48,224},{56,72... | collective-permute-start | bytes 2064392 | tf_op jit(solution)/shard_map/ppermute | solution.py:189
  76.6 31.0 %collective-permute-start.18 = (bf16[12,112,256]{2,1,0:T(8,128)(2,1)}, bf16[12,112,256]{2,1,0:T(8,128)(2,1)S(1)}, u32[]{:S(2)}, u32[]{:S(2)}) collective-permute-start(bf16[12,112,256]{2,1,0:T(8,128)(2,1)} %get-tuple-element.30), channel_id=1, source_target_pairs={{0,208},{8,120},{16,224},{24,72},{32,240},{40,88},{48,192},{56,104... | collective-permute-start | bytes 2064392 | tf_op jit(solution)/shard_map/ppermute | solution.py:189
  76.9 31.6 %collective-permute-start.19 = (bf16[12,112,256]{2,1,0:T(8,128)(2,1)}, bf16[12,112,256]{2,1,0:T(8,128)(2,1)}, u32[]{:S(2)}, u32[]{:S(2)}) collective-permute-start(bf16[12,112,256]{2,1,0:T(8,128)(2,1)} %get-tuple-element.31), channel_id=1, source_target_pairs={{0,128},{8,40},{16,144},{24,56},{32,160},{40,8},{48,176},{56,24},{... | collective-permute-start | bytes 2064392 | tf_op jit(solution)/shard_map/ppermute | solution.py:189
  86.5 49.3 %collective-permute-start.4 = (bf16[12,112,256]{2,1,0:T(8,128)(2,1)}, bf16[12,112,256]{2,1,0:T(8,128)(2,1)}, u32[]{:S(2)}, u32[]{:S(2)}) collective-permute-start(bf16[12,112,256]{2,1,0:T(8,128)(2,1)} %get-tuple-element.25), channel_id=1, source_target_pairs={{0,64},{8,72},{16,80},{24,88},{32,96},{40,104},{48,112},{56,120},{... | collective-permute-start | bytes 2064392 | tf_op jit(solution)/shard_map/ppermute | solution.py:189
  89.8 46.7 %collective-permute-start.5 = (bf16[12,112,256]{2,1,0:T(8,128)(2,1)}, bf16[12,112,256]{2,1,0:T(8,128)(2,1)}, u32[]{:S(2)}, u32[]{:S(2)}) collective-permute-start(bf16[12,112,256]{2,1,0:T(8,128)(2,1)} %get-tuple-element.26), channel_id=1, source_target_pairs={{0,192},{8,200},{16,208},{24,216},{32,224},{40,232},{48,240},{56,2... | collective-permute-start | bytes 2064392 | tf_op jit(solution)/shard_map/ppermute | solution.py:189
  119.5 59.2 %all-to-all-start.1 = ((bf16[8,24,16,128]{3,2,1,0:T(8,128)(2,1)}), bf16[8,24,16,128]{3,2,1,0:T(8,128)(2,1)S(1)}, u32[]{:S(2)}, u32[]{:S(2)}) async-start(bf16[8,24,16,128]{3,2,1,0:T(8,128)(2,1)} %shard_map.87), calls=%async_computation.1 | async-start | bytes 1572864 | tf_op jit(solution)/shard_map/all_to_all | solution.py:198
  124.5 30.1 %collective-permute-start.6 = (bf16[12,112,256]{2,1,0:T(8,128)(2,1)}, bf16[12,112,256]{2,1,0:T(8,128)(2,1)S(1)}, u32[]{:S(2)}, u32[]{:S(2)}) collective-permute-start(bf16[12,112,256]{2,1,0:T(8,128)(2,1)} %get-tuple-element.27), channel_id=1, source_target_pairs={{0,16},{8,24},{16,32},{24,40},{32,48},{40,56},{48,0},{56,8},{64,80... | collective-permute-start | bytes 2064392 | tf_op jit(solution)/shard_map/ppermute | solution.py:189
  127.5 28.6 %collective-permute-start.7 = (bf16[12,112,256]{2,1,0:T(8,128)(2,1)S(1)}, bf16[12,112,256]{2,1,0:T(8,128)(2,1)S(1)}, u32[]{:S(2)}, u32[]{:S(2)}) collective-permute-start(bf16[12,112,256]{2,1,0:T(8,128)(2,1)S(1)} %copy-done.7), channel_id=1, source_target_pairs={{0,48},{8,56},{16,0},{24,8},{32,16},{40,24},{48,32},{56,40},{64,11... | collective-permute-start | bytes 2064392 | tf_op jit(solution)/shard_map/ppermute | solution.py:189
  131.3 37.0 %collective-permute-start.1 = (bf16[12,112,256]{2,1,0:T(8,128)(2,1)S(1)}, bf16[12,112,256]{2,1,0:T(8,128)(2,1)}, u32[]{:S(2)}, u32[]{:S(2)}) collective-permute-start(bf16[12,112,256]{2,1,0:T(8,128)(2,1)S(1)} %copy-done.5), channel_id=1, source_target_pairs={{0,240},{8,88},{16,192},{24,104},{32,208},{40,120},{48,224},{56,72... | collective-permute-start | bytes 2064392 | tf_op jit(solution)/shard_map/ppermute | solution.py:189
  135.8 32.5 %collective-permute-start.2 = (bf16[12,112,256]{2,1,0:T(8,128)(2,1)S(1)}, bf16[12,112,256]{2,1,0:T(8,128)(2,1)}, u32[]{:S(2)}, u32[]{:S(2)}) collective-permute-start(bf16[12,112,256]{2,1,0:T(8,128)(2,1)S(1)} %copy-done.4), channel_id=1, source_target_pairs={{0,208},{8,120},{16,224},{24,72},{32,240},{40,88},{48,192},{56,104... | collective-permute-start | bytes 2064392 | tf_op jit(solution)/shard_map/ppermute | solution.py:189
  136.5 31.7 %collective-permute-start.3 = (bf16[12,112,256]{2,1,0:T(8,128)(2,1)S(1)}, bf16[12,112,256]{2,1,0:T(8,128)(2,1)}, u32[]{:S(2)}, u32[]{:S(2)}) collective-permute-start(bf16[12,112,256]{2,1,0:T(8,128)(2,1)S(1)} %copy-done.3), channel_id=1, source_target_pairs={{0,128},{8,40},{16,144},{24,56},{32,160},{40,8},{48,176},{56,24},{... | collective-permute-start | bytes 2064392 | tf_op jit(solution)/shard_map/ppermute | solution.py:189
  178.7 23.1 %all-to-all-start = ((bf16[8,24,16,128]{3,2,1,0:T(8,128)(2,1)}), bf16[8,24,16,128]{3,2,1,0:T(8,128)(2,1)S(1)}, u32[]{:S(2)}, u32[]{:S(2)}) async-start(bf16[8,24,16,128]{3,2,1,0:T(8,128)(2,1)} %shard_map.84), calls=%async_computation | async-start | bytes 1572864 | tf_op jit(solution)/shard_map/all_to_all | solution.py:198
  185.7 16.1 %collective-permute-start.24 = (f32[24,16,128]{2,1,0:T(8,128)S(1)}, f32[24,16,128]{2,1,0:T(8,128)S(1)}, u32[]{:S(2)}, u32[]{:S(2)}) collective-permute-start(f32[24,16,128]{2,1,0:T(8,128)S(1)} %convert_reduce_fusion), channel_id=1, source_target_pairs={{0,160},{8,168},{16,176},{24,184},{32,128},{40,136},{48,144},{56,1... | collective-permute-start | bytes 589832 | tf_op jit(solution)/shard_map/ppermute | solution.py:201
  (18 other events, 180.7 us)

commit v4 on v3

--- a/solution.py
+++ b/solution.py
@@ -11,7 +11,8 @@
 
 SIDE = 4
 TOGETHER = 3
-BATCHES = ((5, 3), (5, 3))
+COLLECT_VMEM, SUM_VMEM = 14 << 20, 16 << 20
+BATCHES = ((5, 3), (4, 4))
 
 STEPS = (
     ((0, 0), (1, 0), (-1, 0), (0, 1), (0, -1), (-1, -1), (-1, 1), (2, 0)),
@@ -58,6 +59,7 @@
         out_shape=[block] * steps,
         in_specs=[pl.BlockSpec(memory_space=pltpu.SMEM), vmem, vmem],
         out_specs=[vmem] * steps,
+        compiler_params=pltpu.CompilerParams(vmem_limit_bytes=COLLECT_VMEM),
     )(rows, panels, sibling)
 
 
@@ -149,6 +151,7 @@
         out_shape=jax.ShapeDtypeStruct(shape, dtype),
         in_specs=[pl.BlockSpec(memory_space=pltpu.SMEM)] * len(scalars) + [vmem] * len(operands),
         out_specs=vmem,
+        compiler_params=pltpu.CompilerParams(vmem_limit_bytes=SUM_VMEM),
         scratch_shapes=[] if origins is None else [pltpu.VMEM((n, v + r, r), coeffs[0].dtype)],
         cost_estimate=pl.CostEstimate(
             flops=n * rows * r * (4 * v + 2 * r), bytes_accessed=2 * rows * 6 * v + 4 * n * r * r, transcendentals=0

time: 206 us -> 198 us (0.961)
  the two profiles are of different devices: /device:TPU:12 before, /device:TPU:2 now
where the time goes in v4:
time: 198 us; the launch traced here: 197 us
  waiting for transfers between devices  80.7 us (41%)
  starting transfers between devices  57 us (29%)
  Pallas kernels  43.1 us (22%)
  local copies, waits for them, and re-layouts  14.3 us (7%)
  other arithmetic  2.07 us (1%)
    pallas_call x4, Pallas kernels, accumulate(): pl.pallas_call(functools.partial(kernel if origins is None else joint_ker...  35.9 us
    ppermute x14, waiting for transfers between devices, per_device(): row.append(lax.ppermute(blocks[step], 'pairs', perms[step]))  30.7 us
    ppermute x14, starting transfers between devices, per_device(): row.append(lax.ppermute(blocks[step], 'pairs', perms[step]))  19.5 us
    ppermute x4, waiting for transfers between devices, per_device(): lax.ppermute(up, 'aux', [(at, (at + 1) % pieces) for at in range(pieces)])  18.1 us
    all_to_all x2, waiting for transfers between devices, sums(): got = lax.all_to_all(total, 'aux', split_axis=0, concat_axis=0, tiled=True)  13.1 us
    all_to_all x2, starting transfers between devices, sums(): got = lax.all_to_all(total, 'aux', split_axis=0, concat_axis=0, tiled=True)  11.9 us
    unnamed x47, local copies, waits for them, and re-layouts  11.1 us
    ppermute x3, starting transfers between devices, per_device(): lax.ppermute(down, 'aux', [(at, (at - 1) % pieces) for at in range(pieces)])  10.5 us
  transfers between devices with their start and end apart: 27, of which 8 were waited for; matrix products, arithmetic and copies ran while one was open for 3% of the time, Pallas kernels for 22%

profile of v4, /device:TPU:2, one launch (start us, length us, event | category | flops | bytes accessed | tf_op | source)
XLA Modules:
  0.0 197.4 jit_solution(18065485740201466219)
XLA Ops:
  1.9 4.8 %collective-permute-start.9 = (bf16[3,384,128]{2,1,0:T(8,128)(2,1)S(1)}, bf16[3,384,128]{2,1,0:T(8,128)(2,1)S(1)}, u32[]{:S(2)}, u32[]{:S(2)}) collective-permute-start(bf16[3,384,128]{2,1,0:T(8,128)(2,1)S(1)} %pad_maximum_fusion), channel_id=1, source_target_pairs={{0,160},{8,168},{16,176},{24,184},{32,128},{40,136},{48,144},{56,1... | collective-permute-start | bytes 884744 | tf_op jit(solution)/shard_map/ppermute | solution.py:171
  6.7 8.6 %collective-permute-done.9.refs_0_ = bf16[3,384,128]{2,1,0:T(8,128)(2,1)S(1)} collective-permute-done((bf16[3,384,128]{2,1,0:T(8,128)(2,1)S(1)}, bf16[3,384,128]{2,1,0:T(8,128)(2,1)S(1)}, u32[]{:S(2)}, u32[]{:S(2)}) %collective-permute-start.9) | collective-permute-done | bytes 294944 | tf_op jit(solution)/shard_map/ppermute | solution.py:171
  15.3 1.9 collective-permute-start.10
  17.2 3.9 %collective-permute-start.11 = (bf16[3,384,128]{2,1,0:T(8,128)(2,1)S(1)}, bf16[3,384,128]{2,1,0:T(8,128)(2,1)S(1)}, u32[]{:S(2)}, u32[]{:S(2)}) collective-permute-start(bf16[3,384,128]{2,1,0:T(8,128)(2,1)S(1)} %collective-permute-done.9.refs_0_), channel_id=1, source_target_pairs={{0,7},{1,0},{2,1},{3,2},{4,3},{5,4},{6,5},{7,6},{8,15},{9,8},{10,9... | collective-permute-start | bytes 884744 | tf_op jit(solution)/shard_map/ppermute | solution.py:180
  21.2 6.8 %collective-permute-done.10.refs_1_ = bf16[3,384,128]{2,1,0:T(8,128)(2,1)S(1)} collective-permute-done((bf16[3,384,128]{2,1,0:T(8,128)(2,1)S(1)}, bf16[3,384,128]{2,1,0:T(8,128)(2,1)S(1)}, u32[]{:S(2)}, u32[]{:S(2)}) %collective-permute-start.10) | collective-permute-done | bytes 294944 | tf_op jit(solution)/shard_map/ppermute | solution.py:176
  30.8 3.3 %collective-permute-start.13 = (bf16[3,384,128]{2,1,0:T(8,128)(2,1)S(1)}, bf16[3,384,128]{2,1,0:T(8,128)(2,1)}, u32[]{:S(2)}, u32[]{:S(2)}) collective-permute-start(bf16[3,384,128]{2,1,0:T(8,128)(2,1)S(1)} %collective-permute-done.11.refs_2_), channel_id=1, source_target_pairs={{0,7},{1,0},{2,1},{3,2},{4,3},{5,4},{6,5},{7,6},{8,15},{9,8},{10,9... | collective-permute-start | bytes 884744 | tf_op jit(solution)/shard_map/ppermute | solution.py:180
  34.1 3.2 %collective-permute-done.12.refs_3_ = bf16[3,384,128]{2,1,0:T(8,128)(2,1)} collective-permute-done((bf16[3,384,128]{2,1,0:T(8,128)(2,1)S(1)}, bf16[3,384,128]{2,1,0:T(8,128)(2,1)}, u32[]{:S(2)}, u32[]{:S(2)}) %collective-permute-start.12) | collective-permute-done | bytes 294944 | tf_op jit(solution)/shard_map/ppermute | solution.py:176
  37.3 2.0 %copy-done = bf16[64,112,256]{2,1,0:T(8,128)(2,1)S(1)} copy-done((bf16[64,112,256]{2,1,0:T(8,128)(2,1)S(1)}, bf16[64,112,256]{2,1,0:T(8,128)(2,1)}, u32[]{:S(2)}) %copy-start) | copy-done | bytes 3670040
  39.3 3.5 %shard_map.85 = (bf16[12,112,256]{2,1,0:T(8,128)(2,1)S(1)}, bf16[12,112,256]{2,1,0:T(8,128)(2,1)}, bf16[12,112,256]{2,1,0:T(8,128)(2,1)}, bf16[12,112,256]{2,1,0...) custom-call(s32[8,6]{1,0:T(8,128)S(1)} %get-tuple-element.37.rows_re, ...), custom_call_target="tpu_custom_call" | custom-call | tf_op jit(solution)/shard_map/pallas_call | solution.py:57
  44.7 1.5 collective-permute-start.20
  46.7 3.2 %collective-permute-start.15 = (bf16[3,384,128]{2,1,0:T(8,128)(2,1)}, bf16[3,384,128]{2,1,0:T(8,128)(2,1)}, u32[]{:S(2)}, u32[]{:S(2)}) collective-permute-start(bf16[3,384,128]{2,1,0:T(8,128)(2,1)} %collective-permute-done.13.refs_4_), channel_id=1, source_target_pairs={{0,7},{1,0},{2,1},{3,2},{4,3},{5,4},{6,5},{7,6},{8,15},{9,8},{10,9... | collective-permute-start | bytes 884744 | tf_op jit(solution)/shard_map/ppermute | solution.py:180
  50.0 4.8 %collective-permute-start.8 = (s32[12,4]{1,0:T(8,128)S(1)}, s32[12,4]{1,0:T(8,128)S(1)}, u32[]{:S(2)}, u32[]{:S(2)}) collective-permute-start(s32[12,4]{1,0:T(8,128)S(1)} %copy.14.facts_ref), channel_id=1, source_target_pairs={{0,160},{8,168},{16,176},{24,184},{32,128},{40,136},{48,144},{56,1... | collective-permute-start | bytes 584 | tf_op jit(solution)/shard_map/ppermute | solution.py:173
  54.8 10.3 %collective-permute-done.8.facts_ref = s32[12,4]{1,0:T(8,128)S(1)} collective-permute-done((s32[12,4]{1,0:T(8,128)S(1)}, s32[12,4]{1,0:T(8,128)S(1)}, u32[]{:S(2)}, u32[]{:S(2)}) %collective-permute-start.8) | collective-permute-done | bytes 224 | tf_op jit(solution)/shard_map/ppermute | solution.py:173
  65.9 2.5 %collective-permute-start.23 = (bf16[12,112,256]{2,1,0:T(8,128)(2,1)}, bf16[12,112,256]{2,1,0:T(8,128)(2,1)S(1)}, u32[]{:S(2)}, u32[]{:S(2)}) collective-permute-start(bf16[12,112,256]{2,1,0:T(8,128)(2,1)} %copy-done.11), channel_id=1, source_target_pairs={{0,48},{8,56},{16,0},{24,8},{32,16},{40,24},{48,32},{56,40},{64,11... | collective-permute-start | bytes 2064392 | tf_op jit(solution)/shard_map/ppermute | solution.py:192
  68.3 8.1 %collective-permute-done.16.refs_7_ = bf16[3,384,128]{2,1,0:T(8,128)(2,1)S(1)} collective-permute-done((bf16[3,384,128]{2,1,0:T(8,128)(2,1)}, bf16[3,384,128]{2,1,0:T(8,128)(2,1)S(1)}, u32[]{:S(2)}, u32[]{:S(2)}) %collective-permute-start.16) | collective-permute-done | bytes 294944 | tf_op jit(solution)/shard_map/ppermute | solution.py:176
  77.7 3.2 %collective-permute-start.18 = (bf16[12,112,256]{2,1,0:T(8,128)(2,1)S(1)}, bf16[12,112,256]{2,1,0:T(8,128)(2,1)S(1)}, u32[]{:S(2)}, u32[]{:S(2)}) collective-permute-start(bf16[12,112,256]{2,1,0:T(8,128)(2,1)S(1)} %get-tuple-element.30), channel_id=1, source_target_pairs={{0,208},{8,120},{16,224},{24,72},{32,240},{40,88},{48,192},{56,104... | collective-permute-start | bytes 2064392 | tf_op jit(solution)/shard_map/ppermute | solution.py:192
  81.7 2.0 %copy-done.1 = bf16[64,112,256]{2,1,0:T(8,128)(2,1)S(1)} copy-done((bf16[64,112,256]{2,1,0:T(8,128)(2,1)S(1)}, bf16[64,112,256]{2,1,0:T(8,128)(2,1)}, u32[]{:S(2)}) %copy-start.1) | copy-done | bytes 3670040
  83.8 3.7 %shard_map.82 = (bf16[12,112,256]{2,1,0:T(8,128)(2,1)S(1)}, bf16[12,112,256]{2,1,0:T(8,128)(2,1)}, bf16[12,112,256]{2,1,0:T(8,128)(2,1)}, bf16[12,112,256]{2,1,0...) custom-call(s32[8,6]{1,0:T(8,128)S(1)} %get-tuple-element.38.rows_re, ...), custom_call_target="tpu_custom_call" | custom-call | tf_op jit(solution)/shard_map/pallas_call | solution.py:57
  89.2 13.6 %collective-permute-done.22.refs_11_ = bf16[12,112,256]{2,1,0:T(8,128)(2,1)S(1)} collective-permute-done((bf16[12,112,256]{2,1,0:T(8,128)(2,1)}, bf16[12,112,256]{2,1,0:T(8,128)(2,1)S(1)}, u32[]{:S(2)}, u32[]{:S(2)}) %collective-permute-start.22) | collective-permute-done | bytes 688160 | tf_op jit(solution)/shard_map/ppermute | solution.py:192
  102.8 2.0 %collective-permute-start.6 = (bf16[12,112,256]{2,1,0:T(8,128)(2,1)}, bf16[12,112,256]{2,1,0:T(8,128)(2,1)}, u32[]{:S(2)}, u32[]{:S(2)}) collective-permute-start(bf16[12,112,256]{2,1,0:T(8,128)(2,1)} %get-tuple-element.27), channel_id=1, source_target_pairs={{0,192},{8,200},{16,208},{24,216},{32,224},{40,232},{48,240},{56,2... | collective-permute-start | bytes 2064392 | tf_op jit(solution)/shard_map/ppermute | solution.py:192
  104.8 9.1 %shard_map.86.refs_11_ = f32[24,128,128]{2,1,0:T(8,128)S(1)} custom-call(s32[12,4]{1,0:T(8,128)S(1)} %collective-permute-done.8.facts_ref, s32[8]{0:T(128)S(1)} %and_select_fusion.origins_ref, bf16[3,384,128]{2,1,0:T(8,128)(2,1)S(1)} %collective-permute-done.9.refs_0_, bf16[3,384,128]{2,1,0:T(8,128)(2,1)S(1)} %copy-done.17, ...), custom_call_target="tpu_custom_call" | custom-call | flops 4404019200 | bytes 5013504 | tf_op jit(solution)/shard_map/pallas_call | solution.py:149
  114.0 9.1 %shard_map.87 = bf16[8,24,16,128]{3,2,1,0:T(8,128)(2,1)} custom-call(s32[12,4]{1,0:T(8,128)S(1)} %collective-permute-done.8.facts_ref, s32[8]{0:T(128)S(1)} %and_select_fusion.origins_ref, bf16[3,384,128]{2,1,0:T(8,128)(2,1)S(1)} %collective-permute-done.9.refs_0_, bf16[3,384,128]{2,1,0:T(8,128)(2,1)S(1)} %copy-done.17, bf16[3,384,128]{2,1,0:T(8,128)(2,1)S(1)} %copy-done.19, ...), custom_call_target="tpu_custom_call" | custom-call | flops 2642411520 | bytes 3637248 | tf_op jit(solution)/shard_map/pallas_call | solution.py:149
  123.1 4.8 %all-to-all-start.1 = ((bf16[8,24,16,128]{3,2,1,0:T(8,128)(2,1)}), bf16[8,24,16,128]{3,2,1,0:T(8,128)(2,1)}, u32[]{:S(2)}, u32[]{:S(2)}) async-start(bf16[8,24,16,128]{3,2,1,0:T(8,128)(2,1)} %shard_map.87), calls=%async_computation.1 | async-start | bytes 1572864 | tf_op jit(solution)/shard_map/all_to_all | solution.py:201
  128.1 3.1 %collective-permute-start.1 = (bf16[12,112,256]{2,1,0:T(8,128)(2,1)}, bf16[12,112,256]{2,1,0:T(8,128)(2,1)S(1)}, u32[]{:S(2)}, u32[]{:S(2)}) collective-permute-start(bf16[12,112,256]{2,1,0:T(8,128)(2,1)} %copy-done.8), channel_id=1, source_target_pairs={{0,48},{8,56},{16,0},{24,8},{32,16},{40,24},{48,32},{56,40},{64,11... | collective-permute-start | bytes 2064392 | tf_op jit(solution)/shard_map/ppermute | solution.py:192
  131.2 1.8 collective-permute-start.2
  133.0 2.8 %collective-permute-start.3 = (bf16[12,112,256]{2,1,0:T(8,128)(2,1)}, bf16[12,112,256]{2,1,0:T(8,128)(2,1)S(1)}, u32[]{:S(2)}, u32[]{:S(2)}) collective-permute-start(bf16[12,112,256]{2,1,0:T(8,128)(2,1)} %copy-done.4), channel_id=1, source_target_pairs={{0,208},{8,120},{16,224},{24,72},{32,240},{40,88},{48,192},{56,104... | collective-permute-start | bytes 2064392 | tf_op jit(solution)/shard_map/ppermute | solution.py:192
  135.8 17.1 %collective-permute-done.7.refs_3_ = bf16[12,112,256]{2,1,0:T(8,128)(2,1)S(1)} collective-permute-done((bf16[12,112,256]{2,1,0:T(8,128)(2,1)}, bf16[12,112,256]{2,1,0:T(8,128)(2,1)S(1)}, u32[]{:S(2)}, u32[]{:S(2)}) %collective-permute-start.7) | collective-permute-done | bytes 688160 | tf_op jit(solution)/shard_map/ppermute | solution.py:192
  154.0 8.3 %shard_map.83.refs_4_ = f32[24,128,128]{2,1,0:T(8,128)S(1)} custom-call(s32[12,4]{1,0:T(8,128)S(1)} %copy.14.facts_ref, bf16[24,256,128]{2,1,0:T(8,128)(2,1)S(1)} %bitcast.4, bf16[24,128,128]{2,1,0:T(8,128)(2,1)S(1)} %bitcast.7, bf16[12,112,256]{2,1,0:T(8,128)(2,1)S(1)} %copy-done.13, bf16[12,112,256]{2,1,0:T(8,128)(2,1)} %collective-permute-done.5.refs_1_, ...), custom_call_target="tpu_custom_call" | custom-call | flops 3523215360 | bytes 4325376 | tf_op jit(solution)/shard_map/pallas_call | solution.py:149
  162.3 9.4 %shard_map.84 = bf16[8,24,16,128]{3,2,1,0:T(8,128)(2,1)} custom-call(s32[12,4]{1,0:T(8,128)S(1)} %copy.14.facts_ref, bf16[24,256,128]{2,1,0:T(8,128)(2,1)S(1)} %bitcast.5, bf16[24,128,128]{2,1,0:T(8,128)(2,1)S(1)} %bitcast.8, bf16[12,112,256]{2,1,0:T(8,128)(2,1)S(1)} %collective-permute-done.1.refs_0_, ...), custom_call_target="tpu_custom_call" | custom-call | flops 3523215360 | bytes 4325376 | tf_op jit(solution)/shard_map/pallas_call | solution.py:149
  171.7 7.0 %all-to-all-start = ((bf16[8,24,16,128]{3,2,1,0:T(8,128)(2,1)}), bf16[8,24,16,128]{3,2,1,0:T(8,128)(2,1)S(1)}, u32[]{:S(2)}, u32[]{:S(2)}) async-start(bf16[8,24,16,128]{3,2,1,0:T(8,128)(2,1)} %shard_map.84), calls=%async_computation | async-start | bytes 1572864 | tf_op jit(solution)/shard_map/all_to_all | solution.py:201
  180.0 3.6 %collective-permute-start.24 = (f32[24,16,128]{2,1,0:T(8,128)S(1)}, f32[24,16,128]{2,1,0:T(8,128)S(1)}, u32[]{:S(2)}, u32[]{:S(2)}) collective-permute-start(f32[24,16,128]{2,1,0:T(8,128)S(1)} %convert_reduce_fusion), channel_id=1, source_target_pairs={{0,160},{8,168},{16,176},{24,184},{32,128},{40,136},{48,144},{56,1... | collective-permute-start | bytes 589832 | tf_op jit(solution)/shard_map/ppermute | solution.py:204
  183.5 13.1 %all-to-all-done = bf16[8,24,16,128]{3,2,1,0:T(8,128)(2,1)S(1)} async-done(((bf16[8,24,16,128]{3,2,1,0:T(8,128)(2,1)}), bf16[8,24,16,128]{3,2,1,0:T(8,128)(2,1)S(1)}, u32[]{:S(2)}, u32[]{:S(2)}) %all-to-all-start) | async-done | bytes 786464 | tf_op jit(solution)/shard_map/all_to_all | solution.py:201
  (89 shorter events, 15.0 us)
Async XLA Ops:
  0.0 37.3 %collective-permute-start = (bf16[64,112,256]{2,1,0:T(8,128)(2,1)}, bf16[64,112,256]{2,1,0:T(8,128)(2,1)}, u32[]{:S(2)}, u32[]{:S(2)}) collective-permute-start(bf16[64,112,256]{2,1,0:T(8,128)(2,1)} %panels_ref.3), channel_id=1, source_target_pairs={{0,8},{8,0},{16,24},{24,16},{32,40},{40,32},{48,56},{56,48},{64,72... | collective-permute-start | bytes 11010056 | tf_op jit(solution)/shard_map/ppermute | solution.py:169
  1.9 13.4 %collective-permute-start.9 = (bf16[3,384,128]{2,1,0:T(8,128)(2,1)S(1)}, bf16[3,384,128]{2,1,0:T(8,128)(2,1)S(1)}, u32[]{:S(2)}, u32[]{:S(2)}) collective-permute-start(bf16[3,384,128]{2,1,0:T(8,128)(2,1)S(1)} %pad_maximum_fusion), channel_id=1, source_target_pairs={{0,160},{8,168},{16,176},{24,184},{32,128},{40,136},{48,144},{56,1... | collective-permute-start | bytes 884744 | tf_op jit(solution)/shard_map/ppermute | solution.py:171
  15.3 12.7 %collective-permute-start.10 = (bf16[3,384,128]{2,1,0:T(8,128)(2,1)S(1)}, bf16[3,384,128]{2,1,0:T(8,128)(2,1)S(1)}, u32[]{:S(2)}, u32[]{:S(2)}) collective-permute-start(bf16[3,384,128]{2,1,0:T(8,128)(2,1)S(1)} %collective-permute-done.9.refs_0_), channel_id=1, source_target_pairs={{0,1},{1,2},{2,3},{3,4},{4,5},{5,6},{6,7},{7,0},{8,9},{9,10},{10,1... | collective-permute-start | bytes 884744 | tf_op jit(solution)/shard_map/ppermute | solution.py:176
  17.2 13.6 %collective-permute-start.11 = (bf16[3,384,128]{2,1,0:T(8,128)(2,1)S(1)}, bf16[3,384,128]{2,1,0:T(8,128)(2,1)S(1)}, u32[]{:S(2)}, u32[]{:S(2)}) collective-permute-start(bf16[3,384,128]{2,1,0:T(8,128)(2,1)S(1)} %collective-permute-done.9.refs_0_), channel_id=1, source_target_pairs={{0,7},{1,0},{2,1},{3,2},{4,3},{5,4},{6,5},{7,6},{8,15},{9,8},{10,9... | collective-permute-start | bytes 884744 | tf_op jit(solution)/shard_map/ppermute | solution.py:180
  28.0 9.3 %collective-permute-start.12 = (bf16[3,384,128]{2,1,0:T(8,128)(2,1)S(1)}, bf16[3,384,128]{2,1,0:T(8,128)(2,1)}, u32[]{:S(2)}, u32[]{:S(2)}) collective-permute-start(bf16[3,384,128]{2,1,0:T(8,128)(2,1)S(1)} %collective-permute-done.10.refs_1_), channel_id=1, source_target_pairs={{0,1},{1,2},{2,3},{3,4},{4,5},{5,6},{6,7},{7,0},{8,9},{9,10},{10,1... | collective-permute-start | bytes 884744 | tf_op jit(solution)/shard_map/ppermute | solution.py:176
  30.8 15.9 %collective-permute-start.13 = (bf16[3,384,128]{2,1,0:T(8,128)(2,1)S(1)}, bf16[3,384,128]{2,1,0:T(8,128)(2,1)}, u32[]{:S(2)}, u32[]{:S(2)}) collective-permute-start(bf16[3,384,128]{2,1,0:T(8,128)(2,1)S(1)} %collective-permute-done.11.refs_2_), channel_id=1, source_target_pairs={{0,7},{1,0},{2,1},{3,2},{4,3},{5,4},{6,5},{7,6},{8,15},{9,8},{10,9... | collective-permute-start | bytes 884744 | tf_op jit(solution)/shard_map/ppermute | solution.py:180
  37.3 28.6 %collective-permute-start.14 = (bf16[3,384,128]{2,1,0:T(8,128)(2,1)}, bf16[3,384,128]{2,1,0:T(8,128)(2,1)}, u32[]{:S(2)}, u32[]{:S(2)}) collective-permute-start(bf16[3,384,128]{2,1,0:T(8,128)(2,1)} %collective-permute-done.12.refs_3_), channel_id=1, source_target_pairs={{0,1},{1,2},{2,3},{3,4},{4,5},{5,6},{6,7},{7,0},{8,9},{9,10},{10,1... | collective-permute-start | bytes 884744 | tf_op jit(solution)/shard_map/ppermute | solution.py:176
  39.3 42.4 %copy-start.22 = (s32[8]{0:T(128)S(1)}, s32[8]{0:T(128)}, u32[]{:S(2)}) copy-start(s32[8]{0:T(128)} %constant.37.clone) | copy-start | bytes 100
  44.7 32.2 %collective-permute-start.20 = (bf16[12,112,256]{2,1,0:T(8,128)(2,1)}, bf16[12,112,256]{2,1,0:T(8,128)(2,1)S(1)}, u32[]{:S(2)}, u32[]{:S(2)}) collective-permute-start(bf16[12,112,256]{2,1,0:T(8,128)(2,1)} %get-tuple-element.33), channel_id=1, source_target_pairs={{0,64},{8,72},{16,80},{24,88},{32,96},{40,104},{48,112},{56,120},{... | collective-permute-start | bytes 2064392 | tf_op jit(solution)/shard_map/ppermute | solution.py:192
  46.2 34.7 %collective-permute-start.21 = (bf16[12,112,256]{2,1,0:T(8,128)(2,1)}, bf16[12,112,256]{2,1,0:T(8,128)(2,1)}, u32[]{:S(2)}, u32[]{:S(2)}) collective-permute-start(bf16[12,112,256]{2,1,0:T(8,128)(2,1)} %get-tuple-element.34), channel_id=1, source_target_pairs={{0,192},{8,200},{16,208},{24,216},{32,224},{40,232},{48,240},{56,2... | collective-permute-start | bytes 2064392 | tf_op jit(solution)/shard_map/ppermute | solution.py:192
  46.7 21.6 %collective-permute-start.15 = (bf16[3,384,128]{2,1,0:T(8,128)(2,1)}, bf16[3,384,128]{2,1,0:T(8,128)(2,1)}, u32[]{:S(2)}, u32[]{:S(2)}) collective-permute-start(bf16[3,384,128]{2,1,0:T(8,128)(2,1)} %collective-permute-done.13.refs_4_), channel_id=1, source_target_pairs={{0,7},{1,0},{2,1},{3,2},{4,3},{5,4},{6,5},{7,6},{8,15},{9,8},{10,9... | collective-permute-start | bytes 884744 | tf_op jit(solution)/shard_map/ppermute | solution.py:180
  50.0 15.0 %collective-permute-start.8 = (s32[12,4]{1,0:T(8,128)S(1)}, s32[12,4]{1,0:T(8,128)S(1)}, u32[]{:S(2)}, u32[]{:S(2)}) collective-permute-start(s32[12,4]{1,0:T(8,128)S(1)} %copy.14.facts_ref), channel_id=1, source_target_pairs={{0,160},{8,168},{16,176},{24,184},{32,128},{40,136},{48,144},{56,1... | collective-permute-start | bytes 584 | tf_op jit(solution)/shard_map/ppermute | solution.py:173
  65.1 37.7 %collective-permute-start.22 = (bf16[12,112,256]{2,1,0:T(8,128)(2,1)}, bf16[12,112,256]{2,1,0:T(8,128)(2,1)S(1)}, u32[]{:S(2)}, u32[]{:S(2)}) collective-permute-start(bf16[12,112,256]{2,1,0:T(8,128)(2,1)} %copy-done.15), channel_id=1, source_target_pairs={{0,16},{8,24},{16,32},{24,40},{32,48},{40,56},{48,0},{56,8},{64,80... | collective-permute-start | bytes 2064392 | tf_op jit(solution)/shard_map/ppermute | solution.py:192
  65.9 36.9 %collective-permute-start.23 = (bf16[12,112,256]{2,1,0:T(8,128)(2,1)}, bf16[12,112,256]{2,1,0:T(8,128)(2,1)S(1)}, u32[]{:S(2)}, u32[]{:S(2)}) collective-permute-start(bf16[12,112,256]{2,1,0:T(8,128)(2,1)} %copy-done.11), channel_id=1, source_target_pairs={{0,48},{8,56},{16,0},{24,8},{32,16},{40,24},{48,32},{56,40},{64,11... | collective-permute-start | bytes 2064392 | tf_op jit(solution)/shard_map/ppermute | solution.py:192
  68.3 8.1 %collective-permute-start.16 = (bf16[3,384,128]{2,1,0:T(8,128)(2,1)}, bf16[3,384,128]{2,1,0:T(8,128)(2,1)S(1)}, u32[]{:S(2)}, u32[]{:S(2)}) collective-permute-start(bf16[3,384,128]{2,1,0:T(8,128)(2,1)} %collective-permute-done.14.refs_5_), channel_id=1, source_target_pairs={{0,1},{1,2},{2,3},{3,4},{4,5},{5,6},{6,7},{7,0},{8,9},{9,10},{10,1... | collective-permute-start | bytes 884744 | tf_op jit(solution)/shard_map/ppermute | solution.py:176
  76.5 37.4 %collective-permute-start.17 = (bf16[12,112,256]{2,1,0:T(8,128)(2,1)S(1)}, bf16[12,112,256]{2,1,0:T(8,128)(2,1)S(1)}, u32[]{:S(2)}, u32[]{:S(2)}) collective-permute-start(bf16[12,112,256]{2,1,0:T(8,128)(2,1)S(1)} %get-tuple-element.29), channel_id=1, source_target_pairs={{0,240},{8,88},{16,192},{24,104},{32,208},{40,120},{48,224},{56,72... | collective-permute-start | bytes 2064392 | tf_op jit(solution)/shard_map/ppermute | solution.py:192
  77.7 36.2 %collective-permute-start.18 = (bf16[12,112,256]{2,1,0:T(8,128)(2,1)S(1)}, bf16[12,112,256]{2,1,0:T(8,128)(2,1)S(1)}, u32[]{:S(2)}, u32[]{:S(2)}) collective-permute-start(bf16[12,112,256]{2,1,0:T(8,128)(2,1)S(1)} %get-tuple-element.30), channel_id=1, source_target_pairs={{0,208},{8,120},{16,224},{24,72},{32,240},{40,88},{48,192},{56,104... | collective-permute-start | bytes 2064392 | tf_op jit(solution)/shard_map/ppermute | solution.py:192
  80.9 33.0 %collective-permute-start.19 = (bf16[12,112,256]{2,1,0:T(8,128)(2,1)S(1)}, bf16[12,112,256]{2,1,0:T(8,128)(2,1)S(1)}, u32[]{:S(2)}, u32[]{:S(2)}) collective-permute-start(bf16[12,112,256]{2,1,0:T(8,128)(2,1)S(1)} %get-tuple-element.31), channel_id=1, source_target_pairs={{0,128},{8,40},{16,144},{24,56},{32,160},{40,8},{48,176},{56,24},{... | collective-permute-start | bytes 2064392 | tf_op jit(solution)/shard_map/ppermute | solution.py:192
  89.2 24.7 %copy-start.7 = (bf16[12,112,256]{2,1,0:T(8,128)(2,1)}, bf16[12,112,256]{2,1,0:T(8,128)(2,1)S(1)}, u32[]{:S(2)}) copy-start(bf16[12,112,256]{2,1,0:T(8,128)(2,1)S(1)} %get-tuple-element.22) | copy-start | bytes 2064388
  89.2 24.7 %copy-start.8 = (bf16[12,112,256]{2,1,0:T(8,128)(2,1)}, bf16[12,112,256]{2,1,0:T(8,128)(2,1)S(1)}, u32[]{:S(2)}) copy-start(bf16[12,112,256]{2,1,0:T(8,128)(2,1)S(1)} %get-tuple-element.21) | copy-start | bytes 2064388
  102.8 30.3 %collective-permute-start.5 = (bf16[12,112,256]{2,1,0:T(8,128)(2,1)}, bf16[12,112,256]{2,1,0:T(8,128)(2,1)}, u32[]{:S(2)}, u32[]{:S(2)}) collective-permute-start(bf16[12,112,256]{2,1,0:T(8,128)(2,1)} %get-tuple-element.26), channel_id=1, source_target_pairs={{0,64},{8,72},{16,80},{24,88},{32,96},{40,104},{48,112},{56,120},{... | collective-permute-start | bytes 2064392 | tf_op jit(solution)/shard_map/ppermute | solution.py:192
  102.8 33.0 %collective-permute-start.6 = (bf16[12,112,256]{2,1,0:T(8,128)(2,1)}, bf16[12,112,256]{2,1,0:T(8,128)(2,1)}, u32[]{:S(2)}, u32[]{:S(2)}) collective-permute-start(bf16[12,112,256]{2,1,0:T(8,128)(2,1)} %get-tuple-element.27), channel_id=1, source_target_pairs={{0,192},{8,200},{16,208},{24,216},{32,224},{40,232},{48,240},{56,2... | collective-permute-start | bytes 2064392 | tf_op jit(solution)/shard_map/ppermute | solution.py:192
  113.9 38.9 %copy-start.3 = (bf16[12,2,128,128]{3,2,1,0:T(8,128)(2,1)S(1)}, bf16[12,2,128,128]{3,2,1,0:T(8,128)(2,1)}, u32[]{:S(2)}) copy-start(bf16[12,2,128,128]{3,2,1,0:T(8,128)(2,1)} %param.13) | copy-start | bytes 2359300
  123.1 29.8 %copy-start.2 = (bf16[12,2,256,128]{3,2,1,0:T(8,128)(2,1)S(1)}, bf16[12,2,256,128]{3,2,1,0:T(8,128)(2,1)}, u32[]{:S(2)}) copy-start(bf16[12,2,256,128]{3,2,1,0:T(8,128)(2,1)} %param.12) | copy-start | bytes 4718596
  123.1 48.6 %all-to-all-start.1 = ((bf16[8,24,16,128]{3,2,1,0:T(8,128)(2,1)}), bf16[8,24,16,128]{3,2,1,0:T(8,128)(2,1)}, u32[]{:S(2)}, u32[]{:S(2)}) async-start(bf16[8,24,16,128]{3,2,1,0:T(8,128)(2,1)} %shard_map.87), calls=%async_computation.1 | async-start | bytes 1572864 | tf_op jit(solution)/shard_map/all_to_all | solution.py:201
  127.9 24.9 %collective-permute-start.7 = (bf16[12,112,256]{2,1,0:T(8,128)(2,1)}, bf16[12,112,256]{2,1,0:T(8,128)(2,1)S(1)}, u32[]{:S(2)}, u32[]{:S(2)}) collective-permute-start(bf16[12,112,256]{2,1,0:T(8,128)(2,1)} %copy-done.14), channel_id=1, source_target_pairs={{0,16},{8,24},{16,32},{24,40},{32,48},{40,56},{48,0},{56,8},{64,80... | collective-permute-start | bytes 2064392 | tf_op jit(solution)/shard_map/ppermute | solution.py:192
  128.1 34.2 %collective-permute-start.1 = (bf16[12,112,256]{2,1,0:T(8,128)(2,1)}, bf16[12,112,256]{2,1,0:T(8,128)(2,1)S(1)}, u32[]{:S(2)}, u32[]{:S(2)}) collective-permute-start(bf16[12,112,256]{2,1,0:T(8,128)(2,1)} %copy-done.8), channel_id=1, source_target_pairs={{0,48},{8,56},{16,0},{24,8},{32,16},{40,24},{48,32},{56,40},{64,11... | collective-permute-start | bytes 2064392 | tf_op jit(solution)/shard_map/ppermute | solution.py:192
  131.2 31.1 %collective-permute-start.2 = (bf16[12,112,256]{2,1,0:T(8,128)(2,1)}, bf16[12,112,256]{2,1,0:T(8,128)(2,1)S(1)}, u32[]{:S(2)}, u32[]{:S(2)}) collective-permute-start(bf16[12,112,256]{2,1,0:T(8,128)(2,1)} %copy-done.7), channel_id=1, source_target_pairs={{0,240},{8,88},{16,192},{24,104},{32,208},{40,120},{48,224},{56,72... | collective-permute-start | bytes 2064392 | tf_op jit(solution)/shard_map/ppermute | solution.py:192
  133.0 29.3 %collective-permute-start.3 = (bf16[12,112,256]{2,1,0:T(8,128)(2,1)}, bf16[12,112,256]{2,1,0:T(8,128)(2,1)S(1)}, u32[]{:S(2)}, u32[]{:S(2)}) collective-permute-start(bf16[12,112,256]{2,1,0:T(8,128)(2,1)} %copy-done.4), channel_id=1, source_target_pairs={{0,208},{8,120},{16,224},{24,72},{32,240},{40,88},{48,192},{56,104... | collective-permute-start | bytes 2064392 | tf_op jit(solution)/shard_map/ppermute | solution.py:192
  135.8 26.5 %collective-permute-start.4 = (bf16[12,112,256]{2,1,0:T(8,128)(2,1)S(1)}, bf16[12,112,256]{2,1,0:T(8,128)(2,1)S(1)}, u32[]{:S(2)}, u32[]{:S(2)}) collective-permute-start(bf16[12,112,256]{2,1,0:T(8,128)(2,1)S(1)} %get-tuple-element.24), channel_id=1, source_target_pairs={{0,128},{8,40},{16,144},{24,56},{32,160},{40,8},{48,176},{56,24},{... | collective-permute-start | bytes 2064392 | tf_op jit(solution)/shard_map/ppermute | solution.py:192
  171.7 24.9 %all-to-all-start = ((bf16[8,24,16,128]{3,2,1,0:T(8,128)(2,1)}), bf16[8,24,16,128]{3,2,1,0:T(8,128)(2,1)S(1)}, u32[]{:S(2)}, u32[]{:S(2)}) async-start(bf16[8,24,16,128]{3,2,1,0:T(8,128)(2,1)} %shard_map.84), calls=%async_computation | async-start | bytes 1572864 | tf_op jit(solution)/shard_map/all_to_all | solution.py:201
  180.0 16.7 %collective-permute-start.24 = (f32[24,16,128]{2,1,0:T(8,128)S(1)}, f32[24,16,128]{2,1,0:T(8,128)S(1)}, u32[]{:S(2)}, u32[]{:S(2)}) collective-permute-start(f32[24,16,128]{2,1,0:T(8,128)S(1)} %convert_reduce_fusion), channel_id=1, source_target_pairs={{0,160},{8,168},{16,176},{24,184},{32,128},{40,136},{48,144},{56,1... | collective-permute-start | bytes 589832 | tf_op jit(solution)/shard_map/ppermute | solution.py:204
  (18 other events, 157.6 us)
